TPU v7x, 128 devices: a whole 4x4x4 slice. The times are simulated.
128 devices in a mesh: section: 4 (over y), wide: 8 (over z, x_hi), narrow: 4 (over x_lo, core).
Axes of the slice: x: 4 (x_hi: 2, x_lo: 2; x = x_hi * 2 + x_lo), y: 4, z: 4, core: 2. Of those that a mesh axis runs over, the one named last changes fastest.
Arguments:
- normed_inputs: bfloat16 [4, 4, 4, 768, 4096], P('section', 'narrow', None, 'wide'), may hold values from -160 to 160
- value_cotangent: bfloat16 [4, 4, 4, 768, 1024], P('section', 'narrow', None, 'wide'), may hold values from -6 to 6
- expert_hidden: bfloat16 [4, 4, 4, 256, 7168], P('section', 'narrow', None, None, 'wide'), may hold values from -40 to 40
- expert_cotangent: bfloat16 [4, 4, 4, 256, 4096], P('section', 'narrow', None, 'wide'), may hold values from -110 to 110
- slot_gate: bfloat16 [4, 4, 4, 256], P('section', 'narrow', None, 'wide'), may hold values from 0.25 to 1
- slot_count: int32 [4, 4, 4], P('section', 'narrow'), may hold values from 129 to 256, as said below
- expert_weight: bfloat16 [4, 7168, 4096], P('section', 'wide', 'narrow'), may hold values from -0.0625 to 0.0625
- expert_moment: float32 [4, 7168, 4096], P('section', 'wide', 'narrow'), may hold values from -6 to 6
- value_weight: bfloat16 [4, 4096, 1024], P('section', ('wide', 'narrow')), may hold values from -0.09375 to 0.09375
- value_moment: float32 [4, 4096, 1024], P('section', ('wide', 'narrow')), may hold values from -6 to 6
Outputs:
- expert_weight_next: bfloat16 [4, 7168, 4096], P('section', 'wide', 'narrow')
- expert_moment_next: float32 [4, 7168, 4096], P('section', 'wide', 'narrow')
- value_weight_next: bfloat16 [4, 4096, 1024], P('section', ('wide', 'narrow'))
- value_moment_next: float32 [4, 4096, 1024], P('section', ('wide', 'narrow'))
Inputs may be any that keep to these rules, and one draw needn't show every extreme that they name: The live slots of a micro-batch are slots 0 to slot_count - 1; in every layer and replica some micro-batch fills all 256 slots.
All inputs are finite; a program needn't handle non-finite values.
Results may differ from a plain program's by a relative error of at most 0.014.
Values may be sent and summed in bfloat16 or wider, within the bound.
A program may use at most 128 MiB of HBM per device.

v0:
```python
import math

import jax
import jax.numpy as jnp
from jax import lax
from jax.sharding import Mesh
from jax.sharding import PartitionSpec as P

D = 4096
FF = 7168
KV = 1024
WIDE = ("wide_0", "wide_1")
NARROW = ("narrow_0", "narrow_1")
WIDE_NARROW = ("wide_0", "wide_1", "narrow_0", "narrow_1")
SECTION_WIDE_NARROW = ("section", "wide_0", "wide_1", "narrow_0", "narrow_1")


MOMENTUM_DECAY = 0.9
STEP_RATE = 0.01


def over_axes(shard, axes):
    for axis in axes:
        shard = lax.psum(shard, axis)
    return shard


def on_device(
    normed_inputs,
    value_cotangent,
    expert_hidden,
    expert_cotangent,
    slot_gate,
    slot_count,
    expert_weight,
    expert_moment,
    value_weight,
    value_moment,
):
    input_rows = normed_inputs[0, 0].reshape(-1, normed_inputs.shape[-1])
    value_cot_rows = value_cotangent[0, 0].reshape(-1, value_cotangent.shape[-1])
    hidden_local = expert_hidden[0, 0]
    cotangent = expert_cotangent[0, 0]
    gate_local = slot_gate[0, 0]
    live_count = slot_count[0, 0]
    cot_piece = lax.all_gather(cotangent, WIDE, axis=1, tiled=True)
    gate_piece = lax.all_gather(gate_local, WIDE, axis=1, tiled=True)
    length = cot_piece.shape[1]
    positions = jnp.arange(length, dtype=jnp.int32)
    live = positions[None, :] < live_count[:, None]
    coefficient = jnp.where(
        live, gate_piece.astype(jnp.float32), jnp.zeros(gate_piece.shape, jnp.float32)
    )
    scaled = (coefficient[:, :, None] * cot_piece.astype(jnp.float32)).astype(jnp.bfloat16)
    summed = lax.dot_general(
        hidden_local, scaled, (((0, 1), (0, 1)), ((), ())), preferred_element_type=jnp.float32
    )
    expert_grad = lax.psum_scatter(
        summed.astype(jnp.bfloat16), NARROW, scatter_dimension=1, tiled=True
    ).astype(jnp.float32)
    value_grad = lax.psum_scatter(
        lax.dot_general(
            input_rows, value_cot_rows, (((0,), (0,)), ((), ())), preferred_element_type=jnp.float32
        ).astype(jnp.bfloat16),
        WIDE_NARROW,
        scatter_dimension=0,
        tiled=True,
    ).astype(jnp.float32)
    squares = jnp.sum(expert_grad * expert_grad) + jnp.sum(value_grad * value_grad)
    overall = over_axes(squares, SECTION_WIDE_NARROW)
    entry_count = lax.axis_size("section") * (FF * D + D * KV)
    factor = jnp.minimum(1.0, math.sqrt(entry_count) / jnp.sqrt(overall + 1e-06))
    expert_next = MOMENTUM_DECAY * expert_moment[0] + factor * expert_grad
    value_next = MOMENTUM_DECAY * value_moment[0] + factor * value_grad
    expert_weight_next = (expert_weight[0].astype(jnp.float32) - STEP_RATE * expert_next).astype(
        jnp.bfloat16
    )
    value_weight_next = (value_weight[0].astype(jnp.float32) - STEP_RATE * value_next).astype(
        jnp.bfloat16
    )
    return (expert_weight_next[None], expert_next[None], value_weight_next[None], value_next[None])


def solution(mesh):
    finer = Mesh(
        mesh.devices.reshape(mesh.shape["section"], 4, 2, 2, 2),
        ("section", "wide_0", "wide_1", "narrow_0", "narrow_1"),
    )
    in_specs = (
        P("section", NARROW, None, WIDE, None),
        P("section", NARROW, None, WIDE, None),
        P("section", NARROW, None, None, WIDE),
        P("section", NARROW, None, WIDE, None),
        P("section", NARROW, None, WIDE),
        P("section", NARROW, None),
        P("section", WIDE, NARROW),
        P("section", WIDE, NARROW),
        P("section", WIDE_NARROW, None),
        P("section", WIDE_NARROW, None),
    )
    out_specs = (
        P("section", WIDE, NARROW),
        P("section", WIDE, NARROW),
        P("section", WIDE_NARROW, None),
        P("section", WIDE_NARROW, None),
    )
    return jax.shard_map(
        on_device, mesh=finer, in_specs=in_specs, out_specs=out_specs, check_vma=False
    )
```

profile of v0, /device:TPU:1, one launch (start us, length us, event | category | flops | bytes accessed | tf_op | source)
XLA Modules:
  0.0 304.2 jit_solution(16088000934408733016)
XLA Ops:
  8.0 0.0 copy-start
  8.0 0.0 all-gather.4.cloned.1.call-start
  8.1 0.7 all-gather.4.cloned.1.call-update
  8.7 0.0 reduce-scatter.5.cloned.1.call-start
  8.8 1.1 copy-done
  9.9 7.9 %bitcast_convert_fusion = bf16[4096,1024]{1,0:T(8,128)(2,1)} fusion(bf16[1,1,4,96,4096]{4,3,2,1,0:T(8,128)(2,1)S(1)} %copy-done, bf16[1,1,4,96,1024]{4,3,2,1,0:T(8,128)(2,1)} %param.11), kind=kOutput, calls=%fused_computation.2 | convolution fusion | flops 3225419776 | bytes 12320768 | tf_op jit(solution)/shard_map/dot_general | solution.py:62
  17.8 0.0 copy-start.2
  17.8 0.0 copy-start.3
  17.8 0.0 reduce-scatter.5.cloned.1.call-update
  17.8 0.0 reduce-scatter.3.cloned.1.call-start
  17.8 0.6 copy-done.2
  18.4 0.1 copy.21
  18.6 31.8 %all-gather = bf16[1,1,4,256]{2,1,0,3:T(2,128)(2,1)S(1)} all-gather(bf16[1,1,4,32]{2,1,0,3:T(2,128)(2,1)S(1)} %copy.21), channel_id=2, replica_groups=mesh['section'=4,'wide_0'=4,'wide_1'=2,'narrow_0'=2,'narrow_1'=2] {'wide..., dimensions={3}, use_global_device_ids=true | all-gather | bytes 2304 | tf_op jit(solution)/shard_map/all_gather | solution.py:47
  50.3 0.1 convert_element_type.58
  50.5 0.0 copy-done.3
  50.5 0.1 copy.22
  50.6 70.8 %all-gather.4.cloned.1.call-done = bf16[1,1,4,256,4096]{4,3,2,1,0:T(8,128)(2,1)} async-done(((bf16[1,1,4,32,4096]{4,3,2,1,0:T(8,128)(2,1)}), bf16[1,1,4,256,4096]{4,3,2,1,0:T(8,128)(2,1)}) %all-gather.4.cloned.1.call-update) | async-done | bytes 8388624 | tf_op jit(solution)/shard_map/all_gather | solution.py:46
  121.4 14.1 %fusion.5 = bf16[896,4096]{0,1:T(8,128)(2,1)} fusion(bf16[1,1,4,256,4096]{4,3,2,1,0:T(8,128)(2,1)} %all-gather.4.cloned.1.call-done, f32[4,256]{1,0:T(4,128)S(1)} %copy.22, bf16[1,1,4,256,896]{4,3,2,1,0:T(8,128)(2,1)} %param.12), kind=kOutput, calls=%fused_computation.7 | convolution fusion | flops 7532445696 | bytes 17567744 | tf_op jit(solution)/shard_map/dot_general | solution.py:55
  135.6 0.0 reduce-scatter.3.cloned.1.call-update
  135.6 17.6 %reduce-scatter.5.cloned.1.call-done = bf16[128,1024]{1,0:T(8,128)(2,1)} async-done(((bf16[4096,1024]{1,0:T(8,128)(2,1)}), bf16[128,1024]{1,0:T(8,128)(2,1)}) %reduce-scatter.5.cloned.1.call-update) | async-done | bytes 262160 | tf_op jit(solution)/shard_map/reduce_scatter | solution.py:61
  153.2 1.7 fusion.16
  154.9 72.7 %reduce-scatter.3.cloned.1.call-done = bf16[896,1024]{0,1:T(8,128)(2,1)} async-done(((bf16[896,4096]{0,1:T(8,128)(2,1)}), bf16[896,1024]{0,1:T(8,128)(2,1)}) %reduce-scatter.3.cloned.1.call-update) | async-done | bytes 1835024 | tf_op jit(solution)/shard_map/reduce_scatter | solution.py:58
  227.6 3.0 %fusion.8 = f32[]{:T(128)} fusion(bf16[896,1024]{0,1:T(8,128)(2,1)} %reduce-scatter.3.cloned.1.call-done), kind=kLoop, calls=%fused_computation.10 | loop fusion | flops 2752511 | bytes 1835012 | tf_op jit(solution)/shard_map/reduce_sum | solution.py:69
  231.9 9.0 %psum.35 = f32[]{:T(128)} all-reduce(f32[]{:T(128)S(6)} %add.26), channel_id=1, replica_groups=mesh['section'=4,'wide_0'=4,'wide_1'=2,'narrow_0'=2,'narrow_1'=2] {'sect..., use_global_device_ids=true, to_apply=%region_4.5 | all-reduce | flops 1 | bytes 8 | tf_op jit(solution)/shard_map/psum | solution.py:24
  240.9 9.3 %psum.36 = f32[]{:T(128)} all-reduce(f32[]{:T(128)} %psum.35), channel_id=1, replica_groups=mesh['section'=4,'wide_0'=4,'wide_1'=2,'narrow_0'=2,'narrow_1'=2] {'wide..., use_global_device_ids=true, to_apply=%region_5.6 | all-reduce | flops 1 | bytes 8 | tf_op jit(solution)/shard_map/psum | solution.py:24
  250.2 5.9 %psum.37 = f32[]{:T(128)} all-reduce(f32[]{:T(128)} %psum.36), channel_id=1, replica_groups=mesh['section'=4,'wide_0'=4,'wide_1'=2,'narrow_0'=2,'narrow_1'=2] {'wide..., use_global_device_ids=true, to_apply=%region_6.7 | all-reduce | flops 1 | bytes 8 | tf_op jit(solution)/shard_map/psum | solution.py:24
  256.0 5.0 %copy.20 = f32[1,896,1024]{1,2,0:T(8,128)} copy(f32[1,896,1024]{2,1,0:T(8,128)} %param.17) | data formatting | bytes 7340032 | tf_op args[7]
  261.1 4.4 %psum.38 = f32[]{:T(128)} all-reduce(f32[]{:T(128)} %psum.37), channel_id=1, replica_groups=mesh['section'=4,'wide_0'=4,'wide_1'=2,'narrow_0'=2,'narrow_1'=2] {'narr..., use_global_device_ids=true, to_apply=%region_7.8 | all-reduce | flops 1 | bytes 8 | tf_op jit(solution)/shard_map/psum | solution.py:24
  265.4 3.8 %copy.19 = bf16[1,896,1024]{1,2,0:T(8,128)(2,1)} copy(bf16[1,896,1024]{2,1,0:T(8,128)(2,1)} %param.16) | data formatting | bytes 3670016 | tf_op args[6]
  269.2 9.4 %psum.39 = f32[]{:T(128)} all-reduce(f32[]{:T(128)} %psum.38), channel_id=1, replica_groups=mesh['section'=4,'wide_0'=4,'wide_1'=2,'narrow_0'=2,'narrow_1'=2] {'narr..., use_global_device_ids=true, to_apply=%region_8.9 | all-reduce | flops 1 | bytes 8 | tf_op jit(solution)/shard_map/psum | solution.py:24
  279.3 6.5 %fusion.12 = (f32[1,896,1024]{1,2,0:T(8,128)}, bf16[1,896,1024]{1,2,0:T(8,128)(2,1)}) fusion(bf16[896,1024]{0,1:T(8,128)(2,1)} %reduce-scatter.3.cloned.1.call-done, f32[1,896,1024]{1,2,0:T(8,128)} %copy.20, f32[]{:T(128)S(6)} %min_shard_map.3, bf16[1,896,1024]{1,2,0:T(8,128)(2,1)} %copy.19), kind=kLoop, calls=%fused_computation.15 | loop fusion | flops 7340032 | bytes 12845060 | tf_op jit(solution)/shard_map/broadcast_in_dim | solution.py:81
  285.8 3.8 %copy.24 = bf16[1,896,1024]{2,1,0:T(8,128)(2,1)} copy(bf16[1,896,1024]{1,2,0:T(8,128)(2,1)} %get-tuple-element.13) | data formatting | bytes 3670016
  289.6 0.0 copy-start.1
  289.6 5.0 %copy.25 = f32[1,896,1024]{2,1,0:T(8,128)} copy(f32[1,896,1024]{1,2,0:T(8,128)} %get-tuple-element.12) | data formatting | bytes 7340032
  294.6 0.0 copy-done.1
  294.6 2.1 fusion.19
  (1 shorter events, 0.0 us)
Async XLA Ops:
  8.0 1.9 copy-start
  8.0 113.4 %all-gather.4.cloned.1.call-start = ((), (), s32[]{:S(2)}) async-start(), calls=%async_computation.4 | async-start | bytes 9437184 | tf_op jit(solution)/shard_map/all_gather | solution.py:46
  8.7 144.4 %reduce-scatter.5.cloned.1.call-start = ((), (), s32[]{:S(2)}) async-start(), calls=%async_computation.3 | async-start | bytes 8650752 | tf_op jit(solution)/shard_map/reduce_scatter | solution.py:61
  17.8 0.7 copy-start.2
  17.8 32.7 %copy-start.3 = (s32[1,1,4]{2,1,0:T(1,128)S(1)}, s32[1,1,4]{2,1,0:T(1,128)}, u32[]{:S(2)}) copy-start(s32[1,1,4]{2,1,0:T(1,128)} %param.15) | copy-start | bytes 52
  17.8 209.8 %reduce-scatter.3.cloned.1.call-start = ((), (), s32[]{:S(2)}) async-start(), calls=%async_computation.2 | async-start | bytes 9175040 | tf_op jit(solution)/shard_map/reduce_scatter | solution.py:58
  289.6 5.0 %copy-start.1 = (bf16[128,1024]{1,0:T(8,128)(2,1)S(1)}, bf16[128,1024]{1,0:T(8,128)(2,1)}, u32[]{:S(2)}) copy-start(bf16[128,1024]{1,0:T(8,128)(2,1)} %reduce-scatter.5.cloned.1.call-done) | copy-start | bytes 786436
Sparse Core Ops, SparseCore 0:
  11.1 110.2 all-gather.3
Sparse Core Ops, SparseCore 1:
  17.9 135.2 reduce-scatter.4
  155.4 72.1 reduce-scatter.2
where the time goes:
time: 305 us; the launch traced here: 304 us
  waiting for transfers between devices  162 us (53%)
  blocking collectives  69.7 us (23%)
  matrix products  22 us (7%)
  local copies, waits for them, and re-layouts  19.5 us (6%)
  between operations  17.5 us (6%)
  other arithmetic  13.5 us (4%)
    reduce_scatter x1, waiting for transfers between devices, on_device(): lax.psum_scatter(summed.astype(jnp.bfloat16), NARROW, scatter_dimension=1...  72.7 us
    all_gather x1, waiting for transfers between devices, on_device(): cot_piece = lax.all_gather(cotangent, WIDE, axis=1, tiled=True)  70.8 us
    psum x5, blocking collectives, over_axes(): shard = lax.psum(shard, axis)  37.9 us
    all_gather x1, blocking collectives, on_device(): gate_piece = lax.all_gather(gate_local, WIDE, axis=1, tiled=True)  31.8 us
    unnamed x13, local copies, waits for them, and re-layouts  19.4 us
    reduce_scatter x1, waiting for transfers between devices, on_device(): lax.psum_scatter(lax.dot_general(input_rows, value_cot_rows, (((0,), (0,)...  17.6 us
    dot_general x1, matrix products, on_device(): lax.dot_general(hidden_local, scaled, (((0, 1), (0, 1)), ((), ())), prefe...  14.1 us
    dot_general x1, matrix products, on_device(): lax.dot_general(input_rows, value_cot_rows, (((0,), (0,)), ((), ())), pre...  7.87 us
  transfers between devices with their start and end apart: 3, of which 3 were waited for; matrix products, arithmetic and copies ran while one was open for 8% of the time, Pallas kernels for 0%

commit v1 on v0

v1 whole, which is shorter than its diff:
```python
import functools
import math

import jax
import jax.numpy as jnp
from jax import lax
from jax.experimental import pallas as pl
from jax.experimental.pallas import tpu as pltpu
from jax.sharding import Mesh
from jax.sharding import PartitionSpec as P

D = 4096
FF = 7168
KV = 1024
SECTIONS = 4
ENTRY_COUNT = SECTIONS * (FF * D + D * KV)
AXES = ("section", "wide_0", "wide_1", "narrow_0", "narrow_1")
WIDE = ("wide_0", "wide_1")
NARROW = ("narrow_0", "narrow_1")
WIDE_NARROW = ("wide_0", "wide_1", "narrow_0", "narrow_1")
MESH = pl.DeviceIdType.MESH

MOMENTUM_DECAY = 0.9
STEP_RATE = 0.01

PIECES = ((0, 0), (1, 0), (2, 0), (2, 1), (3, 0), (3, 1), (0, 1), (1, 1))
BY_Z1 = (0, 2, 4, 6)
BY_Z3 = (1, 3, 5, 7)


def flip(value, mask):
    if mask == 0:
        return value
    if mask == 1:
        return value + 1 - 2 * (value % 2)
    if mask == 2:
        return (value + 2) % 4
    return 3 - value


def kernel(
    count_ref, gate_ref, inputs, value_cot, hidden, cotangent,
    expert_out, value_out, factor_out,
    staged, gathered, relay, weights, tokens, token_cots, parts, halves, quarters, eighths, last,
    norms,
    local_sem, token_send, token_recv, cot_send, cot_recv, z_send, z_recv, zf_send, zf_recv,
    hid_send, hid_recv, val_send, val_recv, norm_send, norm_recv,
):
    section = lax.axis_index("section")
    z = lax.axis_index("wide_0")
    hi = lax.axis_index("wide_1")
    lo = lax.axis_index("narrow_0")
    core = lax.axis_index("narrow_1")
    x = 2 * hi + lo
    side = (hi, 1 - hi)

    def device(dy=0, dz=0, dx=0, dc=0):
        there = flip(x, dx)
        return (flip(section, dy), flip(z, dz), there // 2, there % 2, 1 - core if dc else core)

    def send(src, dst, send_sem, recv_sem, **where):
        return pltpu.make_async_remote_copy(
            src_ref=src, dst_ref=dst, send_sem=send_sem, recv_sem=recv_sem,
            device_id=device(**where), device_id_type=MESH,
        )

    pending = []

    def start(copy):
        copy.start()
        pending.append(copy)
        return copy

    peers = [dict(dx=i // 2, dc=i % 2) for i in range(1, 8)]
    peers += [dict(dz=i) for i in range(1, 4)] + [dict(dy=i) for i in range(1, 4)]

    cot_loads = []
    for rel in range(4):
        column = (2 * (1 - lo if rel // 2 else lo) + (1 - core if rel % 2 else core)) * 1024
        source = cotangent.at[:, :, pl.ds(pl.multiple_of(column, 1024), 1024)]
        load = pltpu.make_async_copy(source, staged.at[rel], local_sem.at[rel])
        load.start()
        cot_loads.append(load)
    barrier = pltpu.get_barrier_semaphore()
    for peer in peers:
        pl.semaphore_signal(barrier, inc=1, device_id=device(**peer), device_id_type=MESH)
    load_cots = pltpu.make_async_copy(value_cot, token_cots.at[0], local_sem.at[4])
    load_cots.start()
    others = []
    for dx in range(4):
        for dz in range(4):
            block = 2 * (4 * flip(z, dz) + flip(x, dx))
            place = pl.ds((dx * 4 + dz) * 128, 128)
            for which, owner in ((0, core), (1, 1 - core)):
                source = inputs.at[:, pl.ds(pl.multiple_of((block + owner) * 128, 128), 128)]
                if which == 0:
                    pltpu.make_async_copy(source, tokens.at[0, :, place], local_sem.at[5]).start()
                else:
                    others.append((source, place))
    hid_loads = []
    for dz in range(4):
        rows = pl.ds(pl.multiple_of(flip(z, dz) * 64, 64), 64)
        load = pltpu.make_async_copy(hidden.at[:, rows, :], weights.at[0, dz], local_sem.at[6 + dz])
        load.start()
        hid_loads.append(load)

    lanes = lax.broadcasted_iota(jnp.int32, (1, 32), 1) + (2 * z + hi) * 32
    diagonal = lax.broadcasted_iota(jnp.int32, (32, 32), 0) == lax.broadcasted_iota(
        jnp.int32, (32, 32), 1
    )
    columns = []
    for micro in range(4):
        gate = gate_ref[micro : micro + 1, :].astype(jnp.float32)
        row = jnp.where(lanes < count_ref[micro], gate, jnp.zeros_like(gate))
        square = jnp.where(diagonal, jnp.broadcast_to(row, (32, 32)), 0.0)
        columns.append(jnp.sum(square, axis=1, keepdims=True))
    for rel in range(4):
        cot_loads[rel].wait()
        for micro in range(4):
            scaled = (columns[micro] * staged[rel, micro].astype(jnp.float32)).astype(jnp.bfloat16)
            if rel == 0:
                gathered[0, 0, micro, hi] = scaled
            else:
                staged[rel, micro] = scaled

    pl.semaphore_wait(barrier, len(peers))

    def piece(slot, index):
        replica, far = PIECES[index]
        return gathered.at[slot, replica, :, side[far]]

    def along_z(index):
        start(send(piece(0, index), piece(1, index), z_send.at[0, index], z_recv.at[0, index], dz=1))
        start(send(piece(0, index), piece(3, index), z_send.at[1, index], z_recv.at[1, index], dz=3))

    def z_arrival(link, index):
        slot = (1, 3)[link]
        return send(piece(0, index), piece(slot, index), z_send.at[link, index], z_recv.at[link, index], dz=slot)

    def forward_z(index):
        if index in BY_Z1:
            z_arrival(1, index).wait_recv()
            start(send(piece(3, index), piece(2, index), zf_send.at[index], zf_recv.at[index], dz=1))
        else:
            z_arrival(0, index).wait_recv()
            start(send(piece(1, index), piece(2, index), zf_send.at[index], zf_recv.at[index], dz=3))

    def into(replica, far):
        return gathered.at[0, replica, :, side[far]]

    mine_0 = into(0, 0)
    cot = {}

    def cot_send_of(name, index, src, dst, **where):
        cot[name] = start(send(src, dst, cot_send.at[index], cot_recv.at[index], **where))

    cot_send_of("core", 0, staged.at[1], into(1, 0), dc=1)
    cot_send_of("relay_1", 1, mine_0, relay.at[0], dx=1)
    cot_send_of("relay_3", 2, staged.at[1], relay.at[1], dx=3)
    along_z(0)
    cot_send_of("x1_same", 3, staged.at[2], into(2, 0), dx=1)
    cot_send_of("x3_same", 4, staged.at[2], into(2, 0), dx=3)
    cot_send_of("x1_cross", 5, staged.at[3], into(3, 0), dx=1, dc=1)
    cot_send_of("x3_cross", 6, staged.at[3], into(3, 0), dx=3, dc=1)

    for source, place in others:
        send(source, tokens.at[1, :, place], token_send.at[0], token_recv.at[0], dc=1).start()
    token_whole = send(tokens.at[1], tokens.at[1], token_send.at[0], token_recv.at[0], dc=1)
    pending.append(token_whole)
    cots_whole = start(send(value_cot, token_cots.at[1], token_send.at[1], token_recv.at[1], dc=1))
    hid_core = []
    for dz in range(4):
        rows = pl.ds(pl.multiple_of(flip(z, dz) * 64, 64), 64)
        hid_core.append(
            start(send(hidden.at[:, rows, :], weights.at[1, dz], hid_send.at[0, dz], hid_recv.at[0, dz], dc=1))
        )

    cot["core"].wait_recv()
    along_z(1)

    load_cots.wait()
    pltpu.make_async_copy(tokens.at[0], tokens.at[0], local_sem.at[5]).wait()
    token_whole.wait_recv()
    cots_whole.wait_recv()

    def value_parts(dx):
        def block(dz, carry):
            place = pl.ds(pl.multiple_of((dx * 4 + dz) * 128, 128), 128)
            lhs = tokens[:, :, place].reshape(768, 128)
            rhs = token_cots[...].reshape(768, KV)
            product = lax.dot_general(
                lhs, rhs, (((0,), (0,)), ((), ())), preferred_element_type=jnp.float32
            )
            parts[dx, dz] = product.astype(jnp.bfloat16)
            return carry

        lax.fori_loop(0, 4, block, 0)

    value_parts(2)
    cot["relay_1"].wait_recv()
    cot_send_of("far_3", 7, relay.at[0], into(0, 0), dx=3)
    cot["relay_3"].wait_recv()
    cot_send_of("far_1", 8, relay.at[1], into(1, 1), dx=1, dc=1)
    hid_far = []
    for dz in (0, 1, 3, 2):
        hid_loads[dz].wait()
        hid_far.append(
            start(send(weights.at[0, dz], weights.at[2, dz], hid_send.at[1, dz], hid_recv.at[1, dz], dx=1))
        )
    value = {}

    def value_send(name, index, src, dst, **where):
        value[name] = start(send(src, dst, val_send.at[index], val_recv.at[index], **where))

    ORDER = (1, 2, 3, 0)
    value_parts(3)
    for i, dz in enumerate(ORDER):
        value_send(("x3", 1, dz), i, parts.at[2, dz], halves.at[1, dz], dx=3)
    cot["x1_same"].wait_recv()
    along_z(2)
    cot["x3_same"].wait_recv()
    along_z(3)
    value_parts(1)
    for i, dz in enumerate(ORDER):
        value_send(("x3", 0, dz), 4 + i, parts.at[3, dz], halves.at[0, dz], dx=3)
    cot["x1_cross"].wait_recv()
    along_z(4)
    cot["x3_cross"].wait_recv()
    along_z(5)
    value_parts(0)
    forward_z(0)
    forward_z(1)
    cot["far_3"].wait_recv()
    along_z(6)
    cot["far_1"].wait_recv()
    along_z(7)

    def products(slot, replica, first=False):
        def tile(n, carry):
            place = pl.ds(pl.multiple_of(n * 256, 256), 256)
            lhs = weights[replica, slot].reshape(256, 896)
            rhs = gathered[slot, replica, :, :, :, place].reshape(256, 256)
            product = lax.dot_general(
                lhs, rhs, (((0,), (0,)), ((), ())), preferred_element_type=jnp.float32
            )
            if first:
                expert_out[:, place] = product
            else:
                expert_out[:, place] += product
            return carry

        lax.fori_loop(0, 4, tile, 0)

    products(0, 0, first=True)
    hid_core[0].wait_recv()
    products(0, 1)
    forward_z(2)
    forward_z(3)

    def second_step(dz):
        value[("x3", 1, dz)].wait_recv()
        total = parts[1, dz].astype(jnp.float32) + halves[1, dz].astype(jnp.float32)
        parts[1, dz] = total.astype(jnp.bfloat16)

    def second_send(dz):
        value_send(("x1", dz), 8 + dz, parts.at[1, dz], quarters.at[dz], dx=1)

    hid_pass = {}

    def pass_hidden(k):
        dz = (0, 1, 3, 2)[k]
        hid_far[k].wait_recv()
        hid_pass[dz] = start(
            send(weights.at[2, dz], weights.at[3, dz], hid_send.at[2, dz], hid_recv.at[2, dz], dc=1)
        )

    second_step(1)
    pass_hidden(0)
    second_send(1)
    forward_z(4)
    products(0, 2)
    second_step(2)
    forward_z(5)
    second_send(2)
    hid_pass[0].wait_recv()
    products(0, 3)
    second_step(3)
    pass_hidden(1)
    second_send(3)
    forward_z(6)
    forward_z(7)
    second_step(0)
    z_arrival(0, 0).wait_recv()
    z_arrival(0, 6).wait_recv()
    products(1, 0)
    second_send(0)
    hid_core[1].wait_recv()
    products(1, 1)
    z_arrival(1, 1).wait_recv()
    z_arrival(1, 7).wait_recv()
    z_arrival(0, 2).wait_recv()
    products(1, 2)
    hid_pass[1].wait_recv()
    z_arrival(0, 4).wait_recv()
    products(1, 3)
    pass_hidden(2)
    products(3, 0)
    hid_core[3].wait_recv()
    products(3, 1)
    z_arrival(1, 3).wait_recv()
    products(3, 2)
    hid_pass[3].wait_recv()
    z_arrival(1, 5).wait_recv()
    products(3, 3)

    def far_arrival(index):
        if index in BY_Z1:
            send(piece(3, index), piece(2, index), zf_send.at[index], zf_recv.at[index], dz=1).wait_recv()
        else:
            send(piece(1, index), piece(2, index), zf_send.at[index], zf_recv.at[index], dz=3).wait_recv()

    def third_step(dz):
        value[("x3", 0, dz)].wait_recv()
        value[("x1", dz)].wait_recv()
        return (
            parts[0, dz].astype(jnp.float32)
            + halves[0, dz].astype(jnp.float32)
            + quarters[dz].astype(jnp.float32)
        )

    pass_hidden(3)
    far_arrival(2)
    far_arrival(3)
    products(2, 2)
    parts[0, 1] = third_step(1).astype(jnp.bfloat16)
    far_arrival(4)
    far_arrival(5)
    hid_pass[2].wait_recv()
    products(2, 3)
    value_send("z1_0", 12, parts.at[0, 1], eighths.at[0], dz=1)
    parts[0, 2] = third_step(2).astype(jnp.bfloat16)
    far_arrival(0)
    far_arrival(6)
    products(2, 0)
    value_send("z1_1", 13, parts.at[0, 2], eighths.at[1], dz=1)
    hid_core[2].wait_recv()
    far_arrival(1)
    far_arrival(7)
    products(2, 1)

    def squares(ref, rows):
        def tile(i, total):
            chunk = ref[pl.ds(pl.multiple_of(i * 8, 8), 8), :]
            for n in range(8):
                one = chunk[:, n * 128 : (n + 1) * 128]
                total = total + one * one
            return total

        return lax.fori_loop(0, rows // 8, tile, jnp.zeros((8, 128), jnp.float32))

    expert_squares = squares(expert_out, 896)
    third = third_step(3)
    value["z1_1"].wait_recv()
    parts[0, 3] = (third + eighths[1].astype(jnp.float32)).astype(jnp.bfloat16)
    value_send("z3", 14, parts.at[0, 3], last, dz=3)
    near = third_step(0)
    value["z1_0"].wait_recv()
    near = near + eighths[0].astype(jnp.float32)
    value["z3"].wait_recv()
    value_out[...] = near + last[...].astype(jnp.float32)
    norms[0] = expert_squares + squares(value_out, 128)

    base = 0
    slot = 1
    for group in (peers[:7], peers[7:10], peers[10:]):
        copies = []
        for i, peer in enumerate(group):
            copies.append(
                start(
                    send(norms.at[base], norms.at[slot + i], norm_send.at[slot + i], norm_recv.at[slot + i], **peer)
                )
            )
        total = norms[base]
        for i, copy in enumerate(copies):
            copy.wait_recv()
            total = total + norms[slot + i]
        base = slot + len(group)
        norms[base] = total
        slot = base + 1
    overall = jnp.sum(jnp.sum(norms[base], axis=0, keepdims=True), axis=1, keepdims=True)
    overall = jnp.broadcast_to(overall, (8, 128))
    factor_out[...] = jnp.minimum(1.0, math.sqrt(ENTRY_COUNT) / jnp.sqrt(overall + 1e-06))

    for copy in pending:
        copy.wait_send()


def on_device(
    normed_inputs, value_cotangent, expert_hidden, expert_cotangent, slot_gate, slot_count,
    expert_weight, expert_moment, value_weight, value_moment,
):
    bf16 = jnp.bfloat16
    any_space = pl.BlockSpec(memory_space=pl.ANY)
    vmem = pl.BlockSpec(memory_space=pltpu.VMEM)
    dma = pltpu.SemaphoreType.DMA
    expert_grad, value_grad, factor = pl.pallas_call(
        kernel,
        name="gradients",
        out_shape=(
            jax.ShapeDtypeStruct((896, 1024), jnp.float32),
            jax.ShapeDtypeStruct((128, 1024), jnp.float32),
            jax.ShapeDtypeStruct((8, 128), jnp.float32),
        ),
        in_specs=[pl.BlockSpec(memory_space=pltpu.SMEM), vmem] + [any_space] * 4,
        out_specs=(vmem, vmem, vmem),
        scratch_shapes=[
            pltpu.VMEM((4, 4, 32, 1024), bf16),
            pltpu.VMEM((4, 4, 4, 2, 32, 1024), bf16),
            pltpu.VMEM((2, 4, 32, 1024), bf16),
            pltpu.VMEM((4, 4, 4, 64, 896), bf16),
            pltpu.VMEM((2, 384, 2048), bf16),
            pltpu.VMEM((2, 384, 1024), bf16),
            pltpu.VMEM((4, 4, 128, 1024), bf16),
            pltpu.VMEM((2, 4, 128, 1024), bf16),
            pltpu.VMEM((4, 128, 1024), bf16),
            pltpu.VMEM((2, 128, 1024), bf16),
            pltpu.VMEM((128, 1024), bf16),
            pltpu.VMEM((17, 8, 128), jnp.float32),
            dma((10,)),
            dma((2,)), dma((2,)),
            dma((9,)), dma((9,)),
            dma((2, 8)), dma((2, 8)),
            dma((8,)), dma((8,)),
            dma((3, 4)), dma((3, 4)),
            dma((15,)), dma((15,)),
            dma((17,)), dma((17,)),
        ],
        compiler_params=pltpu.CompilerParams(
            collective_id=0, has_side_effects=True, vmem_limit_bytes=46 * 1024 * 1024
        ),
        cost_estimate=pl.CostEstimate(
            flops=2 * 896 * 1024 * 4096 + 2 * 2048 * 1024 * 768,
            bytes_accessed=10_000_000,
            transcendentals=0,
        ),
    )(
        slot_count[0, 0],
        slot_gate[0, 0],
        normed_inputs[0, 0].reshape(384, D),
        value_cotangent[0, 0].reshape(384, KV),
        expert_hidden[0, 0],
        expert_cotangent[0, 0],
    )
    factor = factor[0, 0]
    expert_next = MOMENTUM_DECAY * expert_moment[0] + factor * expert_grad
    value_next = MOMENTUM_DECAY * value_moment[0] + factor * value_grad
    expert_weight_next = (expert_weight[0].astype(jnp.float32) - STEP_RATE * expert_next).astype(bf16)
    value_weight_next = (value_weight[0].astype(jnp.float32) - STEP_RATE * value_next).astype(bf16)
    return (expert_weight_next[None], expert_next[None], value_weight_next[None], value_next[None])


def solution(mesh):
    finer = Mesh(mesh.devices.reshape(mesh.shape["section"], 4, 2, 2, 2), AXES)
    specs = (
        P("section", WIDE, NARROW),
        P("section", WIDE, NARROW),
        P("section", WIDE_NARROW, None),
        P("section", WIDE_NARROW, None),
    )
    in_specs = (
        P("section", NARROW, None, WIDE, None),
        P("section", NARROW, None, WIDE, None),
        P("section", NARROW, None, None, WIDE),
        P("section", NARROW, None, WIDE, None),
        P("section", NARROW, None, WIDE),
        P("section", NARROW, None),
    ) + specs
    return jax.shard_map(
        on_device, mesh=finer, in_specs=in_specs, out_specs=specs, check_vma=False
    )
```

time: 305 us -> 127 us (0.42)
  waiting for transfers between devices: 162 us -> 0 us
  Pallas kernels: 0 us -> 110 us
  blocking collectives: 69.7 us -> 0 us
  matrix products: 22 us -> 0 us
  between operations: 17.5 us -> 0.67 us
  local copies, waits for them, and re-layouts: 19.5 us -> 7.57 us
  other arithmetic: 13.5 us -> 7.82 us
    pallas_call x0 -> x1, Pallas kernels: none -> 110 us  [on_device(): pl.pallas_call(kernel, name='gradients', out_shape=(jax.ShapeDtypeStruct(...]
    reduce_scatter x2 -> x0, waiting for transfers between devices: 90.3 us -> none  [the longest x1 72.7 us: on_device(): lax.psum_scatter(summed.astype(jnp.bfloat16), NARROW, scatter_dimension=1...]
    all_gather x1 -> x0, waiting for transfers between devices: 70.8 us -> none  [on_device(): cot_piece = lax.all_gather(cotangent, WIDE, axis=1, tiled=True)]
    psum x5 -> x0, blocking collectives: 37.9 us -> none  [over_axes(): shard = lax.psum(shard, axis)]
    all_gather x1 -> x0, blocking collectives: 31.8 us -> none  [on_device(): gate_piece = lax.all_gather(gate_local, WIDE, axis=1, tiled=True)]
    dot_general x2 -> x0, matrix products: 22 us -> none  [the longest x1 14.1 us: on_device(): lax.dot_general(hidden_local, scaled, (((0, 1), (0, 1)), ((), ())), prefe...]
    unnamed x13 -> x20, local copies, waits for them, and re-layouts: 19.4 us -> 7.09 us
    reduce_sum x2 -> x0, other arithmetic: 4.74 us -> none  [the longest x1 3.05 us: on_device(): jnp.sum(expert_grad * expert_grad) + jnp.sum(value_grad * value_grad)]
  transfers between devices with their start and end apart: 3 -> 0, of which waited for: 3 -> 0; matrix products, arithmetic and copies ran while one was open for 8% -> 0% of each run, Pallas kernels for 0% -> 0%
where the time goes in v1:
time: 127 us; the launch traced here: 126 us
  Pallas kernels  110 us (87%)
  other arithmetic  7.82 us (6%)
  local copies, waits for them, and re-layouts  7.57 us (6%)
    pallas_call x1, Pallas kernels, on_device(): pl.pallas_call(kernel, name='gradients', out_shape=(jax.ShapeDtypeStruct(...  110 us
    unnamed x20, local copies, waits for them, and re-layouts  7.09 us
    broadcast_in_dim x1, other arithmetic, on_device(): expert_next[None]  6.27 us

profile of v1, /device:TPU:1, one launch (start us, length us, event | category | flops | bytes accessed | tf_op | source)
XLA Modules:
  0.0 126.3 jit_solution(15921233343722320641)
XLA Ops:
  0.6 0.0 copy-start
  0.6 1.9 %copy-done = bf16[1,1,4,96,4096]{4,3,2,1,0:T(8,128)(2,1)S(1)} copy-done((bf16[1,1,4,96,4096]{4,3,2,1,0:T(8,128)(2,1)S(1)}, bf16[1,1,4,96,4096]{4,3,2,1,0:T(8,128)(2,1)}, u32[]{:S(2)}) %copy-start) | copy-done | bytes 3145752
  2.5 0.0 copy-start.1
  2.5 1.5 %copy-done.1 = bf16[1,1,4,256,896]{4,3,2,1,0:T(8,128)(2,1)S(1)} copy-done((bf16[1,1,4,256,896]{4,3,2,1,0:T(8,128)(2,1)S(1)}, bf16[1,1,4,256,896]{4,3,2,1,0:T(8,128)(2,1)}, u32[]{:S(2)}) %copy-start.1) | copy-done | bytes 1835032
  4.0 0.0 copy-start.2
  4.0 1.2 copy-done.2
  5.2 0.0 copy-start.3
  5.3 1.1 copy-done.3
  6.4 0.0 copy-start.4
  6.4 0.7 copy-done.4
  7.1 0.0 copy-start.5
  7.1 0.7 copy-done.5
  7.7 0.0 copy-start.6
  7.7 0.0 copy-start.7
  7.7 110.3 %gradients.1 = (f32[896,1024]{1,0:T(8,128)}, f32[128,1024]{1,0:T(8,128)S(1)}, f32[8,128]{1,0:T(8,128)S(1)}) custom-call(s32[4]{0:T(128)S(1)} %bitcast.38, bf16[4,32]{1,0:T(4,128)(2,1)S(1)} %bitcast.37, bf16[384,4096]{1,0:T(8,128)(2,1)S(1)} %bitcast.33, bf16[384,1024]{1,0:T(8,128)(2,1)S(1)} %bitcast.36, bf16[4,256,896]{2,1,0:T(8,128)(2,1)S(1)} %bitcast.34, ...), custom_call_target="tpu_custom_call" | custom-call | flops 10737418240 | bytes 10000000 | tf_op jit(solution)/shard_map/gradients/pallas_call | solution.py:406
  118.0 0.5 slice.3
  118.5 0.0 copy-done.6
  118.5 0.0 copy-done.7
  118.5 0.0 copy-start.8
  118.5 0.0 copy-start.9
  118.5 6.3 %fusion.2 = (f32[1,896,1024]{2,1,0:T(8,128)}, bf16[1,896,1024]{2,1,0:T(8,128)(2,1)}) fusion(f32[896,1024]{1,0:T(8,128)} %get-tuple-element.8, f32[]{:T(128)} %bitcast.8, f32[1,896,1024]{2,1,0:T(8,128)S(1)} %copy-done.6, bf16[1,896,1024]{2,1,0:T(8,128)(2,1)S(1)} %copy-done.7), kind=kLoop, calls=%fused_computation.4 | loop fusion | flops 6422528 | bytes 14680068 | tf_op jit(solution)/shard_map/broadcast_in_dim | solution.py:459
  124.8 0.0 copy-done.8
  124.8 0.0 copy-done.9
  124.8 1.6 %fusion.5 = (f32[1,128,1024]{2,1,0:T(8,128)}, bf16[1,128,1024]{2,1,0:T(8,128)(2,1)}) fusion(f32[128,1024]{1,0:T(8,128)S(1)} %get-tuple-element.9, f32[]{:T(128)} %bitcast.8, f32[1,128,1024]{2,1,0:T(8,128)S(1)} %copy-done.8, bf16[1,128,1024]{2,1,0:T(8,128)(2,1)S(1)} %copy-done.9), kind=kLoop, calls=%fused_computation.9 | loop fusion | flops 917504 | bytes 2097156 | tf_op jit(solution)/shard_map/broadcast_in_dim | solution.py:459
Async XLA Ops:
  0.6 1.9 %copy-start = (bf16[1,1,4,96,4096]{4,3,2,1,0:T(8,128)(2,1)S(1)}, bf16[1,1,4,96,4096]{4,3,2,1,0:T(8,128)(2,1)}, u32[]{:S(2)}) copy-start(bf16[1,1,4,96,4096]{4,3,2,1,0:T(8,128)(2,1)} %param.10) | copy-start | bytes 9437188
  2.5 1.5 %copy-start.1 = (bf16[1,1,4,256,896]{4,3,2,1,0:T(8,128)(2,1)S(1)}, bf16[1,1,4,256,896]{4,3,2,1,0:T(8,128)(2,1)}, u32[]{:S(2)}) copy-start(bf16[1,1,4,256,896]{4,3,2,1,0:T(8,128)(2,1)} %param.12) | copy-start | bytes 5505028
  4.0 1.2 copy-start.2
  5.2 1.1 copy-start.3
  6.4 0.7 copy-start.4
  7.1 0.7 copy-start.5
  7.7 110.8 %copy-start.6 = (f32[1,896,1024]{2,1,0:T(8,128)S(1)}, f32[1,896,1024]{2,1,0:T(8,128)}, u32[]{:S(2)}) copy-start(f32[1,896,1024]{2,1,0:T(8,128)} %param.17) | copy-start | bytes 11010052
  7.7 110.8 %copy-start.7 = (bf16[1,896,1024]{2,1,0:T(8,128)(2,1)S(1)}, bf16[1,896,1024]{2,1,0:T(8,128)(2,1)}, u32[]{:S(2)}) copy-start(bf16[1,896,1024]{2,1,0:T(8,128)(2,1)} %param.16) | copy-start | bytes 5505028
  118.5 6.3 %copy-start.8 = (f32[1,128,1024]{2,1,0:T(8,128)S(1)}, f32[1,128,1024]{2,1,0:T(8,128)}, u32[]{:S(2)}) copy-start(f32[1,128,1024]{2,1,0:T(8,128)} %param.19) | copy-start | bytes 1572868
  118.5 6.3 %copy-start.9 = (bf16[1,128,1024]{2,1,0:T(8,128)(2,1)S(1)}, bf16[1,128,1024]{2,1,0:T(8,128)(2,1)}, u32[]{:S(2)}) copy-start(bf16[1,128,1024]{2,1,0:T(8,128)(2,1)} %param.18) | copy-start | bytes 786436

commit v2 on v1

--- a/solution.py
+++ b/solution.py
@@ -1,4 +1,3 @@
-import functools
 import math
 
 import jax
@@ -39,9 +38,9 @@
 
 
 def kernel(
-    count_ref, gate_ref, inputs, value_cot, hidden, cotangent,
+    counts, gates, inputs, value_cot, hidden, cotangent,
     expert_out, value_out, factor_out,
-    staged, gathered, relay, weights, tokens, token_cots, parts, halves, quarters, eighths, last,
+    count_ref, gate_ref, staged, gathered, relay, weights, tokens, token_cots, parts, halves, quarters, eighths, last,
     norms,
     local_sem, token_send, token_recv, cot_send, cot_recv, z_send, z_recv, zf_send, zf_recv,
     hid_send, hid_recv, val_send, val_recv, norm_send, norm_recv,
@@ -74,6 +73,12 @@
     peers = [dict(dx=i // 2, dc=i % 2) for i in range(1, 8)]
     peers += [dict(dz=i) for i in range(1, 4)] + [dict(dy=i) for i in range(1, 4)]
 
+    small_loads = [
+        pltpu.make_async_copy(counts, count_ref, local_sem.at[10]),
+        pltpu.make_async_copy(gates, gate_ref, local_sem.at[11]),
+    ]
+    for load in small_loads:
+        load.start()
     cot_loads = []
     for rel in range(4):
         column = (2 * (1 - lo if rel // 2 else lo) + (1 - core if rel % 2 else core)) * 1024
@@ -109,6 +114,8 @@
         jnp.int32, (32, 32), 1
     )
     columns = []
+    for load in small_loads:
+        load.wait()
     for micro in range(4):
         gate = gate_ref[micro : micro + 1, :].astype(jnp.float32)
         row = jnp.where(lanes < count_ref[micro], gate, jnp.zeros_like(gate))
@@ -395,25 +402,66 @@
         copy.wait_send()
 
 
+def update_kernel(
+    factor_ref, expert_grad, expert_moment, expert_weight, value_grad, value_moment, value_weight,
+    expert_weight_out, expert_moment_out, value_weight_out, value_moment_out,
+    new_weights, new_moments, weight_sem, moment_sem,
+):
+    factor = factor_ref[0:1, 0:1]
+    copies = []
+    for tile in range(8):
+        rows = pl.ds(tile * 128, 128)
+        if tile < 7:
+            there, refs = rows, (expert_grad, expert_moment, expert_weight)
+            outs = (expert_weight_out, expert_moment_out)
+        else:
+            there, refs = pl.ds(0, 128), (value_grad, value_moment, value_weight)
+            outs = (value_weight_out, value_moment_out)
+
+        def chunk(i, carry, tile=tile, refs=refs):
+            grad, moment, weight = refs
+            at = pl.ds(pl.multiple_of((tile % 7) * 128 + i * 16, 16), 16)
+            to = pl.ds(pl.multiple_of(tile * 128 + i * 16, 16), 16)
+            moved = MOMENTUM_DECAY * moment[at, :] + factor * grad[at, :]
+            new_moments[to, :] = moved
+            new_weights[to, :] = (weight[at, :].astype(jnp.float32) - STEP_RATE * moved).astype(
+                jnp.bfloat16
+            )
+            return carry
+
+        lax.fori_loop(0, 8, chunk, 0)
+        for src, dst, sem in (
+            (new_weights, outs[0], weight_sem),
+            (new_moments, outs[1], moment_sem),
+        ):
+            copy = pltpu.make_async_copy(src.at[rows, :], dst.at[there, :], sem.at[tile])
+            copy.start()
+            copies.append(copy)
+    for copy in copies:
+        copy.wait()
+
+
 def on_device(
     normed_inputs, value_cotangent, expert_hidden, expert_cotangent, slot_gate, slot_count,
     expert_weight, expert_moment, value_weight, value_moment,
 ):
     bf16 = jnp.bfloat16
-    any_space = pl.BlockSpec(memory_space=pl.ANY)
+    in_hbm = pl.BlockSpec(memory_space=pltpu.HBM)
     vmem = pl.BlockSpec(memory_space=pltpu.VMEM)
     dma = pltpu.SemaphoreType.DMA
     expert_grad, value_grad, factor = pl.pallas_call(
         kernel,
         name="gradients",
         out_shape=(
-            jax.ShapeDtypeStruct((896, 1024), jnp.float32),
-            jax.ShapeDtypeStruct((128, 1024), jnp.float32),
-            jax.ShapeDtypeStruct((8, 128), jnp.float32),
+            pltpu.VMEM((896, 1024), jnp.float32),
+            pltpu.VMEM((128, 1024), jnp.float32),
+            pltpu.VMEM((8, 128), jnp.float32),
         ),
-        in_specs=[pl.BlockSpec(memory_space=pltpu.SMEM), vmem] + [any_space] * 4,
+        in_specs=[in_hbm] * 6,
         out_specs=(vmem, vmem, vmem),
         scratch_shapes=[
+            pltpu.SMEM((4,), jnp.int32),
+            pltpu.VMEM((4, 32), bf16),
             pltpu.VMEM((4, 4, 32, 1024), bf16),
             pltpu.VMEM((4, 4, 4, 2, 32, 1024), bf16),
             pltpu.VMEM((2, 4, 32, 1024), bf16),
@@ -426,7 +474,7 @@
             pltpu.VMEM((2, 128, 1024), bf16),
             pltpu.VMEM((128, 1024), bf16),
             pltpu.VMEM((17, 8, 128), jnp.float32),
-            dma((10,)),
+            dma((12,)),
             dma((2,)), dma((2,)),
             dma((9,)), dma((9,)),
             dma((2, 8)), dma((2, 8)),
@@ -444,18 +492,36 @@
             transcendentals=0,
         ),
     )(
-        slot_count[0, 0],
-        slot_gate[0, 0],
-        normed_inputs[0, 0].reshape(384, D),
-        value_cotangent[0, 0].reshape(384, KV),
-        expert_hidden[0, 0],
-        expert_cotangent[0, 0],
+        pltpu.with_memory_space_constraint(slot_count[0, 0], pltpu.HBM),
+        pltpu.with_memory_space_constraint(slot_gate[0, 0], pltpu.HBM),
+        pltpu.with_memory_space_constraint(normed_inputs[0, 0].reshape(384, D), pltpu.HBM),
+        pltpu.with_memory_space_constraint(value_cotangent[0, 0].reshape(384, KV), pltpu.HBM),
+        pltpu.with_memory_space_constraint(expert_hidden[0, 0], pltpu.HBM),
+        pltpu.with_memory_space_constraint(expert_cotangent[0, 0], pltpu.HBM),
     )
-    factor = factor[0, 0]
-    expert_next = MOMENTUM_DECAY * expert_moment[0] + factor * expert_grad
-    value_next = MOMENTUM_DECAY * value_moment[0] + factor * value_grad
-    expert_weight_next = (expert_weight[0].astype(jnp.float32) - STEP_RATE * expert_next).astype(bf16)
-    value_weight_next = (value_weight[0].astype(jnp.float32) - STEP_RATE * value_next).astype(bf16)
+    expert_weight_next, expert_next, value_weight_next, value_next = pl.pallas_call(
+        update_kernel,
+        name="update",
+        out_shape=(
+            jax.ShapeDtypeStruct((896, 1024), bf16),
+            jax.ShapeDtypeStruct((896, 1024), jnp.float32),
+            jax.ShapeDtypeStruct((128, 1024), bf16),
+            jax.ShapeDtypeStruct((128, 1024), jnp.float32),
+        ),
+        in_specs=[vmem] * 7,
+        out_specs=(in_hbm,) * 4,
+        scratch_shapes=[
+            pltpu.VMEM((1024, 1024), bf16),
+            pltpu.VMEM((1024, 1024), jnp.float32),
+            dma((8,)),
+            dma((8,)),
+        ],
+        compiler_params=pltpu.CompilerParams(vmem_limit_bytes=24 * 1024 * 1024),
+        cost_estimate=pl.CostEstimate(flops=6 * 1024 * 1024, bytes_accessed=6_000_000, transcendentals=0),
+    )(
+        factor, expert_grad, expert_moment[0], expert_weight[0],
+        value_grad, value_moment[0], value_weight[0],
+    )
     return (expert_weight_next[None], expert_next[None], value_weight_next[None], value_next[None])
 
 

time: 127 us -> 112 us (0.88)
  other arithmetic: 7.82 us -> 0 us
  local copies, waits for them, and re-layouts: 7.57 us -> 0.02 us
    broadcast_in_dim x2 -> x0, other arithmetic: 7.82 us -> none  [the longest x1 6.27 us: on_device(): expert_next[None]]
    unnamed x20 -> x8, local copies, waits for them, and re-layouts: 7.09 us -> 0.02 us
    pallas_call x1 -> x2, Pallas kernels: 110 us -> 111 us  [the longest x1 108 us: on_device(): pl.pallas_call(kernel, name='gradients', out_shape=(pltpu.VMEM((896, 1024...]
where the time goes in v2:
time: 112 us
  Pallas kernels  111 us (99%)
    pallas_call x1, Pallas kernels, on_device(): pl.pallas_call(kernel, name='gradients', out_shape=(pltpu.VMEM((896, 1024...  108 us
    pallas_call x1, Pallas kernels, on_device(): pl.pallas_call(update_kernel, name='update', out_shape=(jax.ShapeDtypeStr...  3.15 us

profile of v2, /device:TPU:1, one launch (start us, length us, event | category | flops | bytes accessed | tf_op | source)
XLA Modules:
  0.0 111.8 jit_solution(16198733226853134231)
XLA Ops:
  0.6 0.0 copy-start
  0.6 0.0 copy-start.1
  0.7 0.0 copy-start.2
  0.7 0.0 copy-start.3
  0.7 107.9 %gradients.1 = (f32[896,1024]{1,0:T(8,128)S(1)}, f32[128,1024]{1,0:T(8,128)S(1)}, f32[8,128]{1,0:T(8,128)S(1)}) custom-call(s32[4]{0:T(128)} %bitcast.27, bf16[4,32]{1,0:T(4,128)(2,1)} %bitcast.26, bf16[384,4096]{1,0:T(8,128)(2,1)} %bitcast.19, bf16[384,1024]{1,0:T(8,128)(2,1)} %bitcast.23, bf16[4,256,896]{2,1,0:T(8,128)(2,1)} %bitcast.20, ...), custom_call_target="tpu_custom_call" | custom-call | flops 10737418240 | bytes 10000000 | tf_op jit(solution)/shard_map/gradients/pallas_call | solution.py:452
  108.6 0.0 copy-done
  108.6 0.0 copy-done.1
  108.6 0.0 copy-done.2
  108.6 0.0 copy-done.3
  108.6 3.2 %update.1 = (bf16[896,1024]{1,0:T(8,128)(2,1)}, f32[896,1024]{1,0:T(8,128)}, bf16[128,1024]{1,0:T(8,128)(2,1)}, f32[128,1024]{1,0:T(8,128)}) custom-call(f32[8,128]{1,0:T(8,128)S(1)} %get-tuple-element.11.factor_ref, f32[896,1024]{1,0:T(8,128)S(1)} %get-tuple-element.12.expert_grad, f32[896,1024]{1,0:T(8,128)S(1)} %bitcast.14, ...), custom_call_target="tpu_custom_call" | custom-call | flops 6291456 | bytes 6000000 | tf_op jit(solution)/shard_map/update/pallas_call | solution.py:502
Async XLA Ops:
  0.6 108.0 %copy-start = (f32[1,896,1024]{2,1,0:T(8,128)S(1)}, f32[1,896,1024]{2,1,0:T(8,128)}, u32[]{:S(2)}) copy-start(f32[1,896,1024]{2,1,0:T(8,128)} %param.17) | copy-start | bytes 11010052
  0.6 108.0 %copy-start.1 = (bf16[1,896,1024]{2,1,0:T(8,128)(2,1)S(1)}, bf16[1,896,1024]{2,1,0:T(8,128)(2,1)}, u32[]{:S(2)}) copy-start(bf16[1,896,1024]{2,1,0:T(8,128)(2,1)} %param.16) | copy-start | bytes 5505028
  0.7 108.0 %copy-start.2 = (f32[1,128,1024]{2,1,0:T(8,128)S(1)}, f32[1,128,1024]{2,1,0:T(8,128)}, u32[]{:S(2)}) copy-start(f32[1,128,1024]{2,1,0:T(8,128)} %param.19) | copy-start | bytes 1572868
  0.7 108.0 %copy-start.3 = (bf16[1,128,1024]{2,1,0:T(8,128)(2,1)S(1)}, bf16[1,128,1024]{2,1,0:T(8,128)(2,1)}, u32[]{:S(2)}) copy-start(bf16[1,128,1024]{2,1,0:T(8,128)(2,1)} %param.18) | copy-start | bytes 786436

commit v3 on v2

--- a/solution.py
+++ b/solution.py
@@ -40,7 +40,7 @@
 def kernel(
     counts, gates, inputs, value_cot, hidden, cotangent,
     expert_out, value_out, factor_out,
-    count_ref, gate_ref, staged, gathered, relay, weights, tokens, token_cots, parts, halves, quarters, eighths, last,
+    count_ref, gate_ref, staged, gathered, relay, weights, tokens, token_cots, parts, halves, quarters, cross, eighths, last,
     norms,
     local_sem, token_send, token_recv, cot_send, cot_recv, z_send, z_recv, zf_send, zf_recv,
     hid_send, hid_recv, val_send, val_recv, norm_send, norm_recv,
@@ -71,7 +71,11 @@
         return copy
 
     peers = [dict(dx=i // 2, dc=i % 2) for i in range(1, 8)]
-    peers += [dict(dz=i) for i in range(1, 4)] + [dict(dy=i) for i in range(1, 4)]
+    peers += [dict(dz=i % 4, dy=i // 4) for i in range(1, 16)]
+
+    barrier = pltpu.get_barrier_semaphore()
+    for peer in peers:
+        pl.semaphore_signal(barrier, inc=1, device_id=device(**peer), device_id_type=MESH)
 
     small_loads = [
         pltpu.make_async_copy(counts, count_ref, local_sem.at[10]),
@@ -86,9 +90,6 @@
         load = pltpu.make_async_copy(source, staged.at[rel], local_sem.at[rel])
         load.start()
         cot_loads.append(load)
-    barrier = pltpu.get_barrier_semaphore()
-    for peer in peers:
-        pl.semaphore_signal(barrier, inc=1, device_id=device(**peer), device_id_type=MESH)
     load_cots = pltpu.make_async_copy(value_cot, token_cots.at[0], local_sem.at[4])
     load_cots.start()
     others = []
@@ -121,7 +122,8 @@
         row = jnp.where(lanes < count_ref[micro], gate, jnp.zeros_like(gate))
         square = jnp.where(diagonal, jnp.broadcast_to(row, (32, 32)), 0.0)
         columns.append(jnp.sum(square, axis=1, keepdims=True))
-    for rel in range(4):
+
+    def scale(rel):
         cot_loads[rel].wait()
         for micro in range(4):
             scaled = (columns[micro] * staged[rel, micro].astype(jnp.float32)).astype(jnp.bfloat16)
@@ -130,8 +132,6 @@
             else:
                 staged[rel, micro] = scaled
 
-    pl.semaphore_wait(barrier, len(peers))
-
     def piece(slot, index):
         replica, far = PIECES[index]
         return gathered.at[slot, replica, :, side[far]]
@@ -161,10 +161,15 @@
     def cot_send_of(name, index, src, dst, **where):
         cot[name] = start(send(src, dst, cot_send.at[index], cot_recv.at[index], **where))
 
-    cot_send_of("core", 0, staged.at[1], into(1, 0), dc=1)
+    scale(0)
+    scale(1)
+    pl.semaphore_wait(barrier, len(peers))
+    along_z(0)
     cot_send_of("relay_1", 1, mine_0, relay.at[0], dx=1)
     cot_send_of("relay_3", 2, staged.at[1], relay.at[1], dx=3)
-    along_z(0)
+    cot_send_of("core", 0, staged.at[1], into(1, 0), dc=1)
+    scale(2)
+    scale(3)
     cot_send_of("x1_same", 3, staged.at[2], into(2, 0), dx=1)
     cot_send_of("x3_same", 4, staged.at[2], into(2, 0), dx=3)
     cot_send_of("x1_cross", 5, staged.at[3], into(3, 0), dx=1, dc=1)
@@ -203,40 +208,39 @@
 
         lax.fori_loop(0, 4, block, 0)
 
+    value = {}
+
+    def value_send(name, index, src, dst, **where):
+        value[name] = start(send(src, dst, val_send.at[index], val_recv.at[index], **where))
+
+    hid_far = {}
+
+    def send_hidden(dz):
+        hid_loads[dz].wait()
+        hid_far[dz] = start(
+            send(weights.at[0, dz], weights.at[2, dz], hid_send.at[1, dz], hid_recv.at[1, dz], dx=1)
+        )
+
     value_parts(2)
     cot["relay_1"].wait_recv()
     cot_send_of("far_3", 7, relay.at[0], into(0, 0), dx=3)
     cot["relay_3"].wait_recv()
     cot_send_of("far_1", 8, relay.at[1], into(1, 1), dx=1, dc=1)
-    hid_far = []
-    for dz in (0, 1, 3, 2):
-        hid_loads[dz].wait()
-        hid_far.append(
-            start(send(weights.at[0, dz], weights.at[2, dz], hid_send.at[1, dz], hid_recv.at[1, dz], dx=1))
-        )
-    value = {}
-
-    def value_send(name, index, src, dst, **where):
-        value[name] = start(send(src, dst, val_send.at[index], val_recv.at[index], **where))
-
-    ORDER = (1, 2, 3, 0)
+    for dz in (0, 1, 3):
+        send_hidden(dz)
     value_parts(3)
-    for i, dz in enumerate(ORDER):
-        value_send(("x3", 1, dz), i, parts.at[2, dz], halves.at[1, dz], dx=3)
+    for i, (far, dz) in enumerate(((1, 2), (0, 2), (1, 1), (1, 3), (1, 0), (0, 3), (0, 1), (0, 0))):
+        value_send(("x3", far, dz), i, parts.at[3 - far, dz], halves.at[far, dz], dx=3)
     cot["x1_same"].wait_recv()
     along_z(2)
     cot["x3_same"].wait_recv()
     along_z(3)
     value_parts(1)
-    for i, dz in enumerate(ORDER):
-        value_send(("x3", 0, dz), 4 + i, parts.at[3, dz], halves.at[0, dz], dx=3)
     cot["x1_cross"].wait_recv()
     along_z(4)
     cot["x3_cross"].wait_recv()
     along_z(5)
     value_parts(0)
-    forward_z(0)
-    forward_z(1)
     cot["far_3"].wait_recv()
     along_z(6)
     cot["far_1"].wait_recv()
@@ -258,15 +262,11 @@
 
         lax.fori_loop(0, 4, tile, 0)
 
-    products(0, 0, first=True)
-    hid_core[0].wait_recv()
-    products(0, 1)
-    forward_z(2)
-    forward_z(3)
-
-    def second_step(dz):
+    def second_step(dz, more=None):
         value[("x3", 1, dz)].wait_recv()
         total = parts[1, dz].astype(jnp.float32) + halves[1, dz].astype(jnp.float32)
+        if more is not None:
+            total = total + more[...].astype(jnp.float32)
         parts[1, dz] = total.astype(jnp.bfloat16)
 
     def second_send(dz):
@@ -274,82 +274,92 @@
 
     hid_pass = {}
 
-    def pass_hidden(k):
-        dz = (0, 1, 3, 2)[k]
-        hid_far[k].wait_recv()
+    def pass_hidden(dz):
+        hid_far[dz].wait_recv()
         hid_pass[dz] = start(
             send(weights.at[2, dz], weights.at[3, dz], hid_send.at[2, dz], hid_recv.at[2, dz], dc=1)
         )
 
-    second_step(1)
+    def far_arrival(index):
+        if index in BY_Z1:
+            send(piece(3, index), piece(2, index), zf_send.at[index], zf_recv.at[index], dz=1).wait_recv()
+        else:
+            send(piece(1, index), piece(2, index), zf_send.at[index], zf_recv.at[index], dz=3).wait_recv()
+
+    def third_step(dz):
+        value[("x3", 0, dz)].wait_recv()
+        total = parts[0, dz].astype(jnp.float32) + halves[0, dz].astype(jnp.float32)
+        if dz != 2:
+            value[("x1", dz)].wait_recv()
+            total = total + quarters[dz].astype(jnp.float32)
+        return total
+
+    products(0, 0, first=True)
+    second_step(2)
+    hid_core[0].wait_recv()
+    products(0, 1)
+    value_send("cross", 10, parts.at[1, 2], cross, dz=3)
+    parts[0, 2] = third_step(2).astype(jnp.bfloat16)
+    forward_z(0)
+    forward_z(1)
+    value_send("z1_1", 13, parts.at[0, 2], eighths.at[1], dz=1)
+    forward_z(2)
+    forward_z(3)
+    forward_z(4)
     pass_hidden(0)
-    second_send(1)
-    forward_z(4)
     products(0, 2)
-    second_step(2)
     forward_z(5)
-    second_send(2)
     hid_pass[0].wait_recv()
     products(0, 3)
+    forward_z(6)
+    pass_hidden(1)
     second_step(3)
-    pass_hidden(1)
+    forward_z(7)
     second_send(3)
-    forward_z(6)
-    forward_z(7)
-    second_step(0)
     z_arrival(0, 0).wait_recv()
     z_arrival(0, 6).wait_recv()
     products(1, 0)
-    second_send(0)
+    second_step(0)
+    value["cross"].wait_recv()
+    second_step(1, cross)
     hid_core[1].wait_recv()
-    products(1, 1)
     z_arrival(1, 1).wait_recv()
     z_arrival(1, 7).wait_recv()
+    products(1, 1)
+    second_send(1)
+    send_hidden(2)
+    second_send(0)
     z_arrival(0, 2).wait_recv()
     products(1, 2)
+    pass_hidden(3)
     hid_pass[1].wait_recv()
     z_arrival(0, 4).wait_recv()
     products(1, 3)
-    pass_hidden(2)
+    third = third_step(3)
+    value["z1_1"].wait_recv()
+    parts[0, 3] = (third + eighths[1].astype(jnp.float32)).astype(jnp.bfloat16)
     products(3, 0)
+    value_send("z3", 14, parts.at[0, 3], last, dz=3)
+    parts[0, 1] = third_step(1).astype(jnp.bfloat16)
     hid_core[3].wait_recv()
     products(3, 1)
+    value_send("z1_0", 12, parts.at[0, 1], eighths.at[0], dz=1)
     z_arrival(1, 3).wait_recv()
     products(3, 2)
     hid_pass[3].wait_recv()
     z_arrival(1, 5).wait_recv()
     products(3, 3)
-
-    def far_arrival(index):
-        if index in BY_Z1:
-            send(piece(3, index), piece(2, index), zf_send.at[index], zf_recv.at[index], dz=1).wait_recv()
-        else:
-            send(piece(1, index), piece(2, index), zf_send.at[index], zf_recv.at[index], dz=3).wait_recv()
-
-    def third_step(dz):
-        value[("x3", 0, dz)].wait_recv()
-        value[("x1", dz)].wait_recv()
-        return (
-            parts[0, dz].astype(jnp.float32)
-            + halves[0, dz].astype(jnp.float32)
-            + quarters[dz].astype(jnp.float32)
-        )
-
-    pass_hidden(3)
+    pass_hidden(2)
     far_arrival(2)
     far_arrival(3)
     products(2, 2)
-    parts[0, 1] = third_step(1).astype(jnp.bfloat16)
     far_arrival(4)
     far_arrival(5)
     hid_pass[2].wait_recv()
     products(2, 3)
-    value_send("z1_0", 12, parts.at[0, 1], eighths.at[0], dz=1)
-    parts[0, 2] = third_step(2).astype(jnp.bfloat16)
     far_arrival(0)
     far_arrival(6)
     products(2, 0)
-    value_send("z1_1", 13, parts.at[0, 2], eighths.at[1], dz=1)
     hid_core[2].wait_recv()
     far_arrival(1)
     far_arrival(7)
@@ -366,10 +376,6 @@
         return lax.fori_loop(0, rows // 8, tile, jnp.zeros((8, 128), jnp.float32))
 
     expert_squares = squares(expert_out, 896)
-    third = third_step(3)
-    value["z1_1"].wait_recv()
-    parts[0, 3] = (third + eighths[1].astype(jnp.float32)).astype(jnp.bfloat16)
-    value_send("z3", 14, parts.at[0, 3], last, dz=3)
     near = third_step(0)
     value["z1_0"].wait_recv()
     near = near + eighths[0].astype(jnp.float32)
@@ -379,7 +385,7 @@
 
     base = 0
     slot = 1
-    for group in (peers[:7], peers[7:10], peers[10:]):
+    for group in (peers[:7], peers[7:]):
         copies = []
         for i, peer in enumerate(group):
             copies.append(
@@ -471,9 +477,10 @@
             pltpu.VMEM((4, 4, 128, 1024), bf16),
             pltpu.VMEM((2, 4, 128, 1024), bf16),
             pltpu.VMEM((4, 128, 1024), bf16),
+            pltpu.VMEM((128, 1024), bf16),
             pltpu.VMEM((2, 128, 1024), bf16),
             pltpu.VMEM((128, 1024), bf16),
-            pltpu.VMEM((17, 8, 128), jnp.float32),
+            pltpu.VMEM((25, 8, 128), jnp.float32),
             dma((12,)),
             dma((2,)), dma((2,)),
             dma((9,)), dma((9,)),
@@ -481,7 +488,7 @@
             dma((8,)), dma((8,)),
             dma((3, 4)), dma((3, 4)),
             dma((15,)), dma((15,)),
-            dma((17,)), dma((17,)),
+            dma((24,)), dma((24,)),
         ],
         compiler_params=pltpu.CompilerParams(
             collective_id=0, has_side_effects=True, vmem_limit_bytes=46 * 1024 * 1024

time: 112 us -> 105 us (0.938)
  Pallas kernels: 111 us -> 104 us
    pallas_call x1, Pallas kernels: 108 us -> 101 us  [on_device(): pl.pallas_call(kernel, name='gradients', out_shape=(pltpu.VMEM((896, 1024...]
where the time goes in v3:
time: 105 us
  Pallas kernels  104 us (99%)
    pallas_call x1, Pallas kernels, on_device(): pl.pallas_call(kernel, name='gradients', out_shape=(pltpu.VMEM((896, 1024...  101 us
    pallas_call x1, Pallas kernels, on_device(): pl.pallas_call(update_kernel, name='update', out_shape=(jax.ShapeDtypeStr...  3.15 us

profile of v3, /device:TPU:1, one launch (start us, length us, event | category | flops | bytes accessed | tf_op | source)
XLA Modules:
  0.0 105.2 jit_solution(2722106772733125328)
XLA Ops:
  0.6 0.0 copy-start
  0.6 0.0 copy-start.1
  0.7 0.0 copy-start.2
  0.7 0.0 copy-start.3
  0.7 101.3 %gradients.1 = (f32[896,1024]{1,0:T(8,128)S(1)}, f32[128,1024]{1,0:T(8,128)S(1)}, f32[8,128]{1,0:T(8,128)S(1)}) custom-call(s32[4]{0:T(128)} %bitcast.27, bf16[4,32]{1,0:T(4,128)(2,1)} %bitcast.26, bf16[384,4096]{1,0:T(8,128)(2,1)} %bitcast.19, bf16[384,1024]{1,0:T(8,128)(2,1)} %bitcast.23, bf16[4,256,896]{2,1,0:T(8,128)(2,1)} %bitcast.20, ...), custom_call_target="tpu_custom_call" | custom-call | flops 10737418240 | bytes 10000000 | tf_op jit(solution)/shard_map/gradients/pallas_call | solution.py:458
  102.0 0.0 copy-done
  102.0 0.0 copy-done.1
  102.0 0.0 copy-done.2
  102.0 0.0 copy-done.3
  102.0 3.2 %update.1 = (bf16[896,1024]{1,0:T(8,128)(2,1)}, f32[896,1024]{1,0:T(8,128)}, bf16[128,1024]{1,0:T(8,128)(2,1)}, f32[128,1024]{1,0:T(8,128)}) custom-call(f32[8,128]{1,0:T(8,128)S(1)} %get-tuple-element.11.factor_ref, f32[896,1024]{1,0:T(8,128)S(1)} %get-tuple-element.12.expert_grad, f32[896,1024]{1,0:T(8,128)S(1)} %bitcast.14, ...), custom_call_target="tpu_custom_call" | custom-call | flops 6291456 | bytes 6000000 | tf_op jit(solution)/shard_map/update/pallas_call | solution.py:509
Async XLA Ops:
  0.6 101.4 %copy-start = (f32[1,896,1024]{2,1,0:T(8,128)S(1)}, f32[1,896,1024]{2,1,0:T(8,128)}, u32[]{:S(2)}) copy-start(f32[1,896,1024]{2,1,0:T(8,128)} %param.17) | copy-start | bytes 11010052
  0.6 101.4 %copy-start.1 = (bf16[1,896,1024]{2,1,0:T(8,128)(2,1)S(1)}, bf16[1,896,1024]{2,1,0:T(8,128)(2,1)}, u32[]{:S(2)}) copy-start(bf16[1,896,1024]{2,1,0:T(8,128)(2,1)} %param.16) | copy-start | bytes 5505028
  0.7 101.4 %copy-start.2 = (f32[1,128,1024]{2,1,0:T(8,128)S(1)}, f32[1,128,1024]{2,1,0:T(8,128)}, u32[]{:S(2)}) copy-start(f32[1,128,1024]{2,1,0:T(8,128)} %param.19) | copy-start | bytes 1572868
  0.7 101.4 %copy-start.3 = (bf16[1,128,1024]{2,1,0:T(8,128)(2,1)S(1)}, bf16[1,128,1024]{2,1,0:T(8,128)(2,1)}, u32[]{:S(2)}) copy-start(bf16[1,128,1024]{2,1,0:T(8,128)(2,1)} %param.18) | copy-start | bytes 786436

commit v4 on v3

--- a/solution.py
+++ b/solution.py
@@ -39,7 +39,8 @@
 
 def kernel(
     counts, gates, inputs, value_cot, hidden, cotangent,
-    expert_out, value_out, factor_out,
+    expert_moment, expert_weight, value_moment, value_weight,
+    grads_out, moments_out, weights_out, factor_out,
     count_ref, gate_ref, staged, gathered, relay, weights, tokens, token_cots, parts, halves, quarters, cross, eighths, last,
     norms,
     local_sem, token_send, token_recv, cot_send, cot_recv, z_send, z_recv, zf_send, zf_recv,
@@ -90,6 +91,71 @@
         load = pltpu.make_async_copy(source, staged.at[rel], local_sem.at[rel])
         load.start()
         cot_loads.append(load)
+    lanes = lax.broadcasted_iota(jnp.int32, (1, 32), 1) + (2 * z + hi) * 32
+    diagonal = lax.broadcasted_iota(jnp.int32, (32, 32), 0) == lax.broadcasted_iota(
+        jnp.int32, (32, 32), 1
+    )
+    columns = []
+    for load in small_loads:
+        load.wait()
+    for micro in range(4):
+        gate = gate_ref[micro : micro + 1, :].astype(jnp.float32)
+        row = jnp.where(lanes < count_ref[micro], gate, jnp.zeros_like(gate))
+        square = jnp.where(diagonal, jnp.broadcast_to(row, (32, 32)), 0.0)
+        columns.append(jnp.sum(square, axis=1, keepdims=True))
+
+    def scale(rel):
+        cot_loads[rel].wait()
+        for micro in range(4):
+            scaled = (columns[micro] * staged[rel, micro].astype(jnp.float32)).astype(jnp.bfloat16)
+            if rel == 0:
+                gathered[0, 0, micro, hi] = scaled
+            else:
+                staged[rel, micro] = scaled
+
+    def piece(slot, index):
+        replica, far = PIECES[index]
+        return gathered.at[slot, replica, :, side[far]]
+
+    def along_z(index):
+        start(send(piece(0, index), piece(1, index), z_send.at[0, index], z_recv.at[0, index], dz=1))
+        start(send(piece(0, index), piece(3, index), z_send.at[1, index], z_recv.at[1, index], dz=3))
+
+    def z_arrival(link, index):
+        slot = (1, 3)[link]
+        return send(piece(0, index), piece(slot, index), z_send.at[link, index], z_recv.at[link, index], dz=slot)
+
+    def forward_z(index):
+        if index in BY_Z1:
+            z_arrival(1, index).wait_recv()
+            start(send(piece(3, index), piece(2, index), zf_send.at[index], zf_recv.at[index], dz=1))
+        else:
+            z_arrival(0, index).wait_recv()
+            start(send(piece(1, index), piece(2, index), zf_send.at[index], zf_recv.at[index], dz=3))
+
+    def into(replica, far):
+        return gathered.at[0, replica, :, side[far]]
+
+    mine_0 = into(0, 0)
+    cot = {}
+
+    def cot_send_of(name, index, src, dst, **where):
+        cot[name] = start(send(src, dst, cot_send.at[index], cot_recv.at[index], **where))
+
+    scale(0)
+    scale(2)
+    pl.semaphore_wait(barrier, len(peers))
+    along_z(0)
+    scale(1)
+    cot_send_of("x1_same", 3, staged.at[2], into(2, 0), dx=1)
+    cot_send_of("x3_same", 4, staged.at[2], into(2, 0), dx=3)
+    cot_send_of("relay_1", 1, mine_0, relay.at[0], dx=1)
+    scale(3)
+    cot_send_of("core", 0, staged.at[1], into(1, 0), dc=1)
+    cot_send_of("relay_3", 2, staged.at[1], relay.at[1], dx=3)
+    cot_send_of("x1_cross", 5, staged.at[3], into(3, 0), dx=1, dc=1)
+    cot_send_of("x3_cross", 6, staged.at[3], into(3, 0), dx=3, dc=1)
+
     load_cots = pltpu.make_async_copy(value_cot, token_cots.at[0], local_sem.at[4])
     load_cots.start()
     others = []
@@ -105,75 +171,16 @@
                     others.append((source, place))
     hid_loads = []
     for dz in range(4):
-        rows = pl.ds(pl.multiple_of(flip(z, dz) * 64, 64), 64)
-        load = pltpu.make_async_copy(hidden.at[:, rows, :], weights.at[0, dz], local_sem.at[6 + dz])
+        rows = pl.ds(2 * flip(z, dz), 2)
+        load = pltpu.make_async_copy(hidden.at[:, rows], weights.at[0, dz], local_sem.at[6 + dz])
         load.start()
         hid_loads.append(load)
-
-    lanes = lax.broadcasted_iota(jnp.int32, (1, 32), 1) + (2 * z + hi) * 32
-    diagonal = lax.broadcasted_iota(jnp.int32, (32, 32), 0) == lax.broadcasted_iota(
-        jnp.int32, (32, 32), 1
-    )
-    columns = []
-    for load in small_loads:
-        load.wait()
-    for micro in range(4):
-        gate = gate_ref[micro : micro + 1, :].astype(jnp.float32)
-        row = jnp.where(lanes < count_ref[micro], gate, jnp.zeros_like(gate))
-        square = jnp.where(diagonal, jnp.broadcast_to(row, (32, 32)), 0.0)
-        columns.append(jnp.sum(square, axis=1, keepdims=True))
-
-    def scale(rel):
-        cot_loads[rel].wait()
-        for micro in range(4):
-            scaled = (columns[micro] * staged[rel, micro].astype(jnp.float32)).astype(jnp.bfloat16)
-            if rel == 0:
-                gathered[0, 0, micro, hi] = scaled
-            else:
-                staged[rel, micro] = scaled
-
-    def piece(slot, index):
-        replica, far = PIECES[index]
-        return gathered.at[slot, replica, :, side[far]]
-
-    def along_z(index):
-        start(send(piece(0, index), piece(1, index), z_send.at[0, index], z_recv.at[0, index], dz=1))
-        start(send(piece(0, index), piece(3, index), z_send.at[1, index], z_recv.at[1, index], dz=3))
-
-    def z_arrival(link, index):
-        slot = (1, 3)[link]
-        return send(piece(0, index), piece(slot, index), z_send.at[link, index], z_recv.at[link, index], dz=slot)
-
-    def forward_z(index):
-        if index in BY_Z1:
-            z_arrival(1, index).wait_recv()
-            start(send(piece(3, index), piece(2, index), zf_send.at[index], zf_recv.at[index], dz=1))
-        else:
-            z_arrival(0, index).wait_recv()
-            start(send(piece(1, index), piece(2, index), zf_send.at[index], zf_recv.at[index], dz=3))
-
-    def into(replica, far):
-        return gathered.at[0, replica, :, side[far]]
-
-    mine_0 = into(0, 0)
-    cot = {}
-
-    def cot_send_of(name, index, src, dst, **where):
-        cot[name] = start(send(src, dst, cot_send.at[index], cot_recv.at[index], **where))
-
-    scale(0)
-    scale(1)
-    pl.semaphore_wait(barrier, len(peers))
-    along_z(0)
-    cot_send_of("relay_1", 1, mine_0, relay.at[0], dx=1)
-    cot_send_of("relay_3", 2, staged.at[1], relay.at[1], dx=3)
-    cot_send_of("core", 0, staged.at[1], into(1, 0), dc=1)
-    scale(2)
-    scale(3)
-    cot_send_of("x1_same", 3, staged.at[2], into(2, 0), dx=1)
-    cot_send_of("x3_same", 4, staged.at[2], into(2, 0), dx=3)
-    cot_send_of("x1_cross", 5, staged.at[3], into(3, 0), dx=1, dc=1)
-    cot_send_of("x3_cross", 6, staged.at[3], into(3, 0), dx=3, dc=1)
+    state_loads = [
+        pltpu.make_async_copy(expert_moment, moments_out.at[0:896], local_sem.at[12]),
+        pltpu.make_async_copy(expert_weight, weights_out.at[0:896], local_sem.at[13]),
+        pltpu.make_async_copy(value_moment, moments_out.at[896:1024], local_sem.at[14]),
+        pltpu.make_async_copy(value_weight, weights_out.at[896:1024], local_sem.at[15]),
+    ]
 
     for source, place in others:
         send(source, tokens.at[1, :, place], token_send.at[0], token_recv.at[0], dc=1).start()
@@ -182,9 +189,9 @@
     cots_whole = start(send(value_cot, token_cots.at[1], token_send.at[1], token_recv.at[1], dc=1))
     hid_core = []
     for dz in range(4):
-        rows = pl.ds(pl.multiple_of(flip(z, dz) * 64, 64), 64)
+        rows = pl.ds(2 * flip(z, dz), 2)
         hid_core.append(
-            start(send(hidden.at[:, rows, :], weights.at[1, dz], hid_send.at[0, dz], hid_recv.at[0, dz], dc=1))
+            start(send(hidden.at[:, rows], weights.at[1, dz], hid_send.at[0, dz], hid_recv.at[0, dz], dc=1))
         )
 
     cot["core"].wait_recv()
@@ -222,19 +229,21 @@
         )
 
     value_parts(2)
+    cot["x1_same"].wait_recv()
+    along_z(2)
+    cot["x3_same"].wait_recv()
+    along_z(3)
+    value_parts(3)
     cot["relay_1"].wait_recv()
     cot_send_of("far_3", 7, relay.at[0], into(0, 0), dx=3)
     cot["relay_3"].wait_recv()
     cot_send_of("far_1", 8, relay.at[1], into(1, 1), dx=1, dc=1)
     for dz in (0, 1, 3):
         send_hidden(dz)
-    value_parts(3)
     for i, (far, dz) in enumerate(((1, 2), (0, 2), (1, 1), (1, 3), (1, 0), (0, 3), (0, 1), (0, 0))):
         value_send(("x3", far, dz), i, parts.at[3 - far, dz], halves.at[far, dz], dx=3)
-    cot["x1_same"].wait_recv()
-    along_z(2)
-    cot["x3_same"].wait_recv()
-    along_z(3)
+    for load in state_loads:
+        load.start()
     value_parts(1)
     cot["x1_cross"].wait_recv()
     along_z(4)
@@ -246,21 +255,34 @@
     cot["far_1"].wait_recv()
     along_z(7)
 
-    def products(slot, replica, first=False):
+    def accumulate(weights_of, gathered_of, first=False):
         def tile(n, carry):
             place = pl.ds(pl.multiple_of(n * 256, 256), 256)
-            lhs = weights[replica, slot].reshape(256, 896)
-            rhs = gathered[slot, replica, :, :, :, place].reshape(256, 256)
+            lhs = weights_of().reshape(256, 896)
+            rhs = gathered_of(place).reshape(256, 256)
             product = lax.dot_general(
                 lhs, rhs, (((0,), (0,)), ((), ())), preferred_element_type=jnp.float32
             )
             if first:
-                expert_out[:, place] = product
+                grads_out[0:896, place] = product
             else:
-                expert_out[:, place] += product
+                grads_out[0:896, place] += product
             return carry
 
         lax.fori_loop(0, 4, tile, 0)
+
+    def products(slot, replica, first=False):
+        accumulate(
+            lambda: weights[replica, slot],
+            lambda place: gathered[slot, replica, :, :, :, place],
+            first,
+        )
+
+    def chip_products(slot, far):
+        accumulate(
+            lambda: weights[0:2, slot, :, side[far]],
+            lambda place: gathered[slot, 0:2, :, side[far], :, place],
+        )
 
     def second_step(dz, more=None):
         value[("x3", 1, dz)].wait_recv()
@@ -349,39 +371,45 @@
     hid_pass[3].wait_recv()
     z_arrival(1, 5).wait_recv()
     products(3, 3)
+    hid_core[2].wait_recv()
+    far_arrival(0)
+    far_arrival(1)
+    chip_products(2, 0)
     pass_hidden(2)
     far_arrival(2)
     far_arrival(3)
     products(2, 2)
+    hid_pass[2].wait_recv()
     far_arrival(4)
     far_arrival(5)
-    hid_pass[2].wait_recv()
     products(2, 3)
-    far_arrival(0)
     far_arrival(6)
-    products(2, 0)
-    hid_core[2].wait_recv()
-    far_arrival(1)
     far_arrival(7)
-    products(2, 1)
-
-    def squares(ref, rows):
-        def tile(i, total):
-            chunk = ref[pl.ds(pl.multiple_of(i * 8, 8), 8), :]
-            for n in range(8):
-                one = chunk[:, n * 128 : (n + 1) * 128]
-                total = total + one * one
-            return total
-
-        return lax.fori_loop(0, rows // 8, tile, jnp.zeros((8, 128), jnp.float32))
-
-    expert_squares = squares(expert_out, 896)
+    chip_products(2, 1)
+
+    def squares(first, rows):
+        def tile(i, totals):
+            chunk = grads_out[pl.ds(pl.multiple_of(first + i * 32, 32), 32), :]
+            totals = list(totals)
+            for group in range(4):
+                for n in range(8):
+                    one = chunk[group * 8 : (group + 1) * 8, n * 128 : (n + 1) * 128]
+                    totals[n] = totals[n] + one * one
+            return tuple(totals)
+
+        totals = lax.fori_loop(0, rows // 32, tile, (jnp.zeros((8, 128), jnp.float32),) * 8)
+        return sum(totals[1:], totals[0])
+
+    expert_squares = squares(0, 896)
+    for load in state_loads:
+        load.wait()
     near = third_step(0)
     value["z1_0"].wait_recv()
     near = near + eighths[0].astype(jnp.float32)
     value["z3"].wait_recv()
-    value_out[...] = near + last[...].astype(jnp.float32)
-    norms[0] = expert_squares + squares(value_out, 128)
+    grads_out[896:1024, :] = near + last[...].astype(jnp.float32)
+    norms[0] = expert_squares + squares(896, 128)
+    started = len(pending)
 
     base = 0
     slot = 1
@@ -393,6 +421,9 @@
                     send(norms.at[base], norms.at[slot + i], norm_send.at[slot + i], norm_recv.at[slot + i], **peer)
                 )
             )
+        if base == 0:
+            for copy in pending[:started]:
+                copy.wait_send()
         total = norms[base]
         for i, copy in enumerate(copies):
             copy.wait_recv()
@@ -404,38 +435,32 @@
     overall = jnp.broadcast_to(overall, (8, 128))
     factor_out[...] = jnp.minimum(1.0, math.sqrt(ENTRY_COUNT) / jnp.sqrt(overall + 1e-06))
 
-    for copy in pending:
+    for copy in pending[started:]:
         copy.wait_send()
 
 
 def update_kernel(
-    factor_ref, expert_grad, expert_moment, expert_weight, value_grad, value_moment, value_weight,
+    factor_ref, grads, moments, weights,
     expert_weight_out, expert_moment_out, value_weight_out, value_moment_out,
     new_weights, new_moments, weight_sem, moment_sem,
 ):
     factor = factor_ref[0:1, 0:1]
     copies = []
     for tile in range(8):
-        rows = pl.ds(tile * 128, 128)
-        if tile < 7:
-            there, refs = rows, (expert_grad, expert_moment, expert_weight)
-            outs = (expert_weight_out, expert_moment_out)
-        else:
-            there, refs = pl.ds(0, 128), (value_grad, value_moment, value_weight)
-            outs = (value_weight_out, value_moment_out)
-
-        def chunk(i, carry, tile=tile, refs=refs):
-            grad, moment, weight = refs
-            at = pl.ds(pl.multiple_of((tile % 7) * 128 + i * 16, 16), 16)
-            to = pl.ds(pl.multiple_of(tile * 128 + i * 16, 16), 16)
-            moved = MOMENTUM_DECAY * moment[at, :] + factor * grad[at, :]
-            new_moments[to, :] = moved
-            new_weights[to, :] = (weight[at, :].astype(jnp.float32) - STEP_RATE * moved).astype(
+
+        def chunk(i, carry, tile=tile):
+            at = pl.ds(pl.multiple_of(tile * 128 + i * 32, 32), 32)
+            moved = MOMENTUM_DECAY * moments[at, :] + factor * grads[at, :]
+            new_moments[at, :] = moved
+            new_weights[at, :] = (weights[at, :].astype(jnp.float32) - STEP_RATE * moved).astype(
                 jnp.bfloat16
             )
             return carry
 
-        lax.fori_loop(0, 8, chunk, 0)
+        lax.fori_loop(0, 4, chunk, 0)
+        rows = pl.ds(tile * 128, 128)
+        there = rows if tile < 7 else pl.ds(0, 128)
+        outs = (expert_weight_out, expert_moment_out) if tile < 7 else (value_weight_out, value_moment_out)
         for src, dst, sem in (
             (new_weights, outs[0], weight_sem),
             (new_moments, outs[1], moment_sem),
@@ -455,23 +480,24 @@
     in_hbm = pl.BlockSpec(memory_space=pltpu.HBM)
     vmem = pl.BlockSpec(memory_space=pltpu.VMEM)
     dma = pltpu.SemaphoreType.DMA
-    expert_grad, value_grad, factor = pl.pallas_call(
+    grads, moments, weights, factor = pl.pallas_call(
         kernel,
         name="gradients",
         out_shape=(
-            pltpu.VMEM((896, 1024), jnp.float32),
-            pltpu.VMEM((128, 1024), jnp.float32),
+            pltpu.VMEM((1024, 1024), jnp.float32),
+            pltpu.VMEM((1024, 1024), jnp.float32),
+            pltpu.VMEM((1024, 1024), bf16),
             pltpu.VMEM((8, 128), jnp.float32),
         ),
-        in_specs=[in_hbm] * 6,
-        out_specs=(vmem, vmem, vmem),
+        in_specs=[in_hbm] * 10,
+        out_specs=(vmem,) * 4,
         scratch_shapes=[
             pltpu.SMEM((4,), jnp.int32),
             pltpu.VMEM((4, 32), bf16),
             pltpu.VMEM((4, 4, 32, 1024), bf16),
             pltpu.VMEM((4, 4, 4, 2, 32, 1024), bf16),
             pltpu.VMEM((2, 4, 32, 1024), bf16),
-            pltpu.VMEM((4, 4, 4, 64, 896), bf16),
+            pltpu.VMEM((4, 4, 4, 2, 32, 896), bf16),
             pltpu.VMEM((2, 384, 2048), bf16),
             pltpu.VMEM((2, 384, 1024), bf16),
             pltpu.VMEM((4, 4, 128, 1024), bf16),
@@ -481,7 +507,7 @@
             pltpu.VMEM((2, 128, 1024), bf16),
             pltpu.VMEM((128, 1024), bf16),
             pltpu.VMEM((25, 8, 128), jnp.float32),
-            dma((12,)),
+            dma((16,)),
             dma((2,)), dma((2,)),
             dma((9,)), dma((9,)),
             dma((2, 8)), dma((2, 8)),
@@ -503,8 +529,12 @@
         pltpu.with_memory_space_constraint(slot_gate[0, 0], pltpu.HBM),
         pltpu.with_memory_space_constraint(normed_inputs[0, 0].reshape(384, D), pltpu.HBM),
         pltpu.with_memory_space_constraint(value_cotangent[0, 0].reshape(384, KV), pltpu.HBM),
-        pltpu.with_memory_space_constraint(expert_hidden[0, 0], pltpu.HBM),
+        pltpu.with_memory_space_constraint(expert_hidden[0, 0].reshape(4, 8, 32, 896), pltpu.HBM),
         pltpu.with_memory_space_constraint(expert_cotangent[0, 0], pltpu.HBM),
+        pltpu.with_memory_space_constraint(expert_moment[0], pltpu.HBM),
+        pltpu.with_memory_space_constraint(expert_weight[0], pltpu.HBM),
+        pltpu.with_memory_space_constraint(value_moment[0], pltpu.HBM),
+        pltpu.with_memory_space_constraint(value_weight[0], pltpu.HBM),
     )
     expert_weight_next, expert_next, value_weight_next, value_next = pl.pallas_call(
         update_kernel,
@@ -515,7 +545,7 @@
             jax.ShapeDtypeStruct((128, 1024), bf16),
             jax.ShapeDtypeStruct((128, 1024), jnp.float32),
         ),
-        in_specs=[vmem] * 7,
+        in_specs=[vmem] * 4,
         out_specs=(in_hbm,) * 4,
         scratch_shapes=[
             pltpu.VMEM((1024, 1024), bf16),
@@ -526,8 +556,7 @@
         compiler_params=pltpu.CompilerParams(vmem_limit_bytes=24 * 1024 * 1024),
         cost_estimate=pl.CostEstimate(flops=6 * 1024 * 1024, bytes_accessed=6_000_000, transcendentals=0),
     )(
-        factor, expert_grad, expert_moment[0], expert_weight[0],
-        value_grad, value_moment[0], value_weight[0],
+        factor, grads, moments, weights,
     )
     return (expert_weight_next[None], expert_next[None], value_weight_next[None], value_next[None])
 

time: 105 us -> 103 us (0.981)
  Pallas kernels: 104 us -> 102 us
    pallas_call x1, Pallas kernels: 101 us -> 99 us  [on_device(): pl.pallas_call(kernel, name='gradients', out_shape=(pltpu.VMEM((1024, 102...]
where the time goes in v4:
time: 103 us
  Pallas kernels  102 us (99%)
    pallas_call x1, Pallas kernels, on_device(): pl.pallas_call(kernel, name='gradients', out_shape=(pltpu.VMEM((1024, 102...  99 us
    pallas_call x1, Pallas kernels, on_device(): pl.pallas_call(update_kernel, name='update', out_shape=(jax.ShapeDtypeStr...  3.05 us

profile of v4, /device:TPU:1, one launch (start us, length us, event | category | flops | bytes accessed | tf_op | source)
XLA Modules:
  0.0 102.7 jit_solution(8387755720036882121)
XLA Ops:
  0.6 99.0 %gradients.1 = (f32[1024,1024]{1,0:T(8,128)S(1)}, f32[1024,1024]{1,0:T(8,128)S(1)}, bf16[1024,1024]{1,0:T(8,128)(2,1)S(1)}, f32[8,128]{1,0:T(8,128)S(1)}) custom-call(s32[4]{0:T(128)} %bitcast.27, bf16[4,32]{1,0:T(4,128)(2,1)} %bitcast.26, bf16[384,4096]{1,0:T(8,128)(2,1)} %bitcast.16, bf16[384,1024]{1,0:T(8,128)(2,1)} %bitcast.21, ...), custom_call_target="tpu_custom_call" | custom-call | flops 10737418240 | bytes 10000000 | tf_op jit(solution)/shard_map/gradients/pallas_call | solution.py:483
  99.6 3.1 %update.1 = (bf16[896,1024]{1,0:T(8,128)(2,1)}, f32[896,1024]{1,0:T(8,128)}, bf16[128,1024]{1,0:T(8,128)(2,1)}, f32[128,1024]{1,0:T(8,128)}) custom-call(f32[8,128]{1,0:T(8,128)S(1)} %get-tuple-element.12.factor_ref, f32[1024,1024]{1,0:T(8,128)S(1)} %get-tuple-element.13.grads, f32[1024,1024]{1,0:T(8,128)S(1)} %get-tuple-element.14.moments, ...), custom_call_target="tpu_custom_call" | custom-call | flops 6291456 | bytes 6000000 | tf_op jit(solution)/shard_map/update/pallas_call | solution.py:539

commit v5 on v4

--- a/solution.py
+++ b/solution.py
@@ -44,7 +44,7 @@
     count_ref, gate_ref, staged, gathered, relay, weights, tokens, token_cots, parts, halves, quarters, cross, eighths, last,
     norms,
     local_sem, token_send, token_recv, cot_send, cot_recv, z_send, z_recv, zf_send, zf_recv,
-    hid_send, hid_recv, val_send, val_recv, norm_send, norm_recv,
+    hid_send, hid_recv, val_send, val_recv, norm_send, norm_recv, reach_sem,
 ):
     section = lax.axis_index("section")
     z = lax.axis_index("wide_0")
@@ -73,10 +73,6 @@
 
     peers = [dict(dx=i // 2, dc=i % 2) for i in range(1, 8)]
     peers += [dict(dz=i % 4, dy=i // 4) for i in range(1, 16)]
-
-    barrier = pltpu.get_barrier_semaphore()
-    for peer in peers:
-        pl.semaphore_signal(barrier, inc=1, device_id=device(**peer), device_id_type=MESH)
 
     small_loads = [
         pltpu.make_async_copy(counts, count_ref, local_sem.at[10]),
@@ -91,6 +87,12 @@
         load = pltpu.make_async_copy(source, staged.at[rel], local_sem.at[rel])
         load.start()
         cot_loads.append(load)
+    barrier = pltpu.get_barrier_semaphore()
+    near = [dict(dc=1), dict(dz=1), dict(dz=3), dict(dy=1), dict(dy=3)]
+    near += [dict(dx=dx, dc=dc) for dx in (1, 3) for dc in (0, 1)]
+    for peer in near:
+        pl.semaphore_signal(barrier, inc=1, device_id=device(**peer), device_id_type=MESH)
+
     lanes = lax.broadcasted_iota(jnp.int32, (1, 32), 1) + (2 * z + hi) * 32
     diagonal = lax.broadcasted_iota(jnp.int32, (32, 32), 0) == lax.broadcasted_iota(
         jnp.int32, (32, 32), 1
@@ -113,6 +115,15 @@
             else:
                 staged[rel, micro] = scaled
 
+    def spread(step):
+        if step:
+            pl.semaphore_wait(reach_sem.at[step - 1], 4)
+        if step < 3:
+            for peer in near[1:5]:
+                pl.semaphore_signal(
+                    reach_sem.at[step], inc=1, device_id=device(**peer), device_id_type=MESH
+                )
+
     def piece(slot, index):
         replica, far = PIECES[index]
         return gathered.at[slot, replica, :, side[far]]
@@ -143,8 +154,8 @@
         cot[name] = start(send(src, dst, cot_send.at[index], cot_recv.at[index], **where))
 
     scale(0)
+    pl.semaphore_wait(barrier, len(near))
     scale(2)
-    pl.semaphore_wait(barrier, len(peers))
     along_z(0)
     scale(1)
     cot_send_of("x1_same", 3, staged.at[2], into(2, 0), dx=1)
@@ -182,6 +193,7 @@
         pltpu.make_async_copy(value_weight, weights_out.at[896:1024], local_sem.at[15]),
     ]
 
+    spread(0)
     for source, place in others:
         send(source, tokens.at[1, :, place], token_send.at[0], token_recv.at[0], dc=1).start()
     token_whole = send(tokens.at[1], tokens.at[1], token_send.at[0], token_recv.at[0], dc=1)
@@ -244,12 +256,14 @@
         value_send(("x3", far, dz), i, parts.at[3 - far, dz], halves.at[far, dz], dx=3)
     for load in state_loads:
         load.start()
+    spread(1)
     value_parts(1)
     cot["x1_cross"].wait_recv()
     along_z(4)
     cot["x3_cross"].wait_recv()
     along_z(5)
     value_parts(0)
+    spread(2)
     cot["far_3"].wait_recv()
     along_z(6)
     cot["far_1"].wait_recv()
@@ -400,6 +414,7 @@
         totals = lax.fori_loop(0, rows // 32, tile, (jnp.zeros((8, 128), jnp.float32),) * 8)
         return sum(totals[1:], totals[0])
 
+    spread(3)
     expert_squares = squares(0, 896)
     for load in state_loads:
         load.wait()
@@ -515,6 +530,7 @@
             dma((3, 4)), dma((3, 4)),
             dma((15,)), dma((15,)),
             dma((24,)), dma((24,)),
+            pltpu.SemaphoreType.REGULAR((3,)),
         ],
         compiler_params=pltpu.CompilerParams(
             collective_id=0, has_side_effects=True, vmem_limit_bytes=46 * 1024 * 1024

time: 103 us -> 102 us (level)
  no operation moved by 1% of the time
where the time goes in v5:
time: 102 us
  Pallas kernels  101 us (99%)
    pallas_call x1, Pallas kernels, on_device(): pl.pallas_call(kernel, name='gradients', out_shape=(pltpu.VMEM((1024, 102...  98 us
    pallas_call x1, Pallas kernels, on_device(): pl.pallas_call(update_kernel, name='update', out_shape=(jax.ShapeDtypeStr...  3.05 us

profile of v5, /device:TPU:1, one launch (start us, length us, event | category | flops | bytes accessed | tf_op | source)
XLA Modules:
  0.0 101.7 jit_solution(4463864054974938153)
XLA Ops:
  0.6 98.0 %gradients.1 = (f32[1024,1024]{1,0:T(8,128)S(1)}, f32[1024,1024]{1,0:T(8,128)S(1)}, bf16[1024,1024]{1,0:T(8,128)(2,1)S(1)}, f32[8,128]{1,0:T(8,128)S(1)}) custom-call(s32[4]{0:T(128)} %bitcast.27, bf16[4,32]{1,0:T(4,128)(2,1)} %bitcast.26, bf16[384,4096]{1,0:T(8,128)(2,1)} %bitcast.16, bf16[384,1024]{1,0:T(8,128)(2,1)} %bitcast.21, ...), custom_call_target="tpu_custom_call" | custom-call | flops 10737418240 | bytes 10000000 | tf_op jit(solution)/shard_map/gradients/pallas_call | solution.py:498
  98.6 3.1 %update.1 = (bf16[896,1024]{1,0:T(8,128)(2,1)}, f32[896,1024]{1,0:T(8,128)}, bf16[128,1024]{1,0:T(8,128)(2,1)}, f32[128,1024]{1,0:T(8,128)}) custom-call(f32[8,128]{1,0:T(8,128)S(1)} %get-tuple-element.12.factor_ref, f32[1024,1024]{1,0:T(8,128)S(1)} %get-tuple-element.13.grads, f32[1024,1024]{1,0:T(8,128)S(1)} %get-tuple-element.14.moments, ...), custom_call_target="tpu_custom_call" | custom-call | flops 6291456 | bytes 6000000 | tf_op jit(solution)/shard_map/update/pallas_call | solution.py:555

commit v6 on v5

--- a/solution.py
+++ b/solution.py
@@ -18,6 +18,8 @@
 NARROW = ("narrow_0", "narrow_1")
 WIDE_NARROW = ("wide_0", "wide_1", "narrow_0", "narrow_1")
 MESH = pl.DeviceIdType.MESH
+
+TILE = 128
 
 MOMENTUM_DECAY = 0.9
 STEP_RATE = 0.01
@@ -71,8 +73,8 @@
         pending.append(copy)
         return copy
 
-    peers = [dict(dx=i // 2, dc=i % 2) for i in range(1, 8)]
-    peers += [dict(dz=i % 4, dy=i // 4) for i in range(1, 16)]
+    row_peers = [dict(dx=dx, dc=dc) for dx, dc in ((2, 1), (2, 0), (1, 1), (3, 1), (1, 0), (3, 0), (0, 1))]
+    far_peers = [dict(dz=i % 4, dy=i // 4) for i in (10, 6, 14, 9, 11, 2, 8, 5, 7, 13, 15, 1, 3, 4, 12)]
 
     small_loads = [
         pltpu.make_async_copy(counts, count_ref, local_sem.at[10]),
@@ -157,10 +159,10 @@
     pl.semaphore_wait(barrier, len(near))
     scale(2)
     along_z(0)
-    scale(1)
     cot_send_of("x1_same", 3, staged.at[2], into(2, 0), dx=1)
     cot_send_of("x3_same", 4, staged.at[2], into(2, 0), dx=3)
     cot_send_of("relay_1", 1, mine_0, relay.at[0], dx=1)
+    scale(1)
     scale(3)
     cot_send_of("core", 0, staged.at[1], into(1, 0), dc=1)
     cot_send_of("relay_3", 2, staged.at[1], relay.at[1], dx=3)
@@ -351,6 +353,7 @@
     pass_hidden(1)
     second_step(3)
     forward_z(7)
+    drained = len(pending)
     second_send(3)
     z_arrival(0, 0).wait_recv()
     z_arrival(0, 6).wait_recv()
@@ -397,6 +400,8 @@
     far_arrival(4)
     far_arrival(5)
     products(2, 3)
+    for copy in pending[:drained]:
+        copy.wait_send()
     far_arrival(6)
     far_arrival(7)
     chip_products(2, 1)
@@ -423,12 +428,12 @@
     near = near + eighths[0].astype(jnp.float32)
     value["z3"].wait_recv()
     grads_out[896:1024, :] = near + last[...].astype(jnp.float32)
-    norms[0] = expert_squares + squares(896, 128)
+    norms[0] = jnp.sum(expert_squares + squares(896, 128), axis=0, keepdims=True)
     started = len(pending)
 
     base = 0
     slot = 1
-    for group in (peers[:7], peers[7:]):
+    for group in (row_peers, far_peers):
         copies = []
         for i, peer in enumerate(group):
             copies.append(
@@ -437,16 +442,16 @@
                 )
             )
         if base == 0:
-            for copy in pending[:started]:
+            for copy in pending[drained:started]:
                 copy.wait_send()
         total = norms[base]
-        for i, copy in enumerate(copies):
+        for i, copy in reversed(tuple(enumerate(copies))):
             copy.wait_recv()
             total = total + norms[slot + i]
         base = slot + len(group)
         norms[base] = total
         slot = base + 1
-    overall = jnp.sum(jnp.sum(norms[base], axis=0, keepdims=True), axis=1, keepdims=True)
+    overall = jnp.sum(norms[base], axis=1, keepdims=True)
     overall = jnp.broadcast_to(overall, (8, 128))
     factor_out[...] = jnp.minimum(1.0, math.sqrt(ENTRY_COUNT) / jnp.sqrt(overall + 1e-06))
 
@@ -461,10 +466,10 @@
 ):
     factor = factor_ref[0:1, 0:1]
     copies = []
-    for tile in range(8):
+    for tile in range(1024 // TILE):
 
         def chunk(i, carry, tile=tile):
-            at = pl.ds(pl.multiple_of(tile * 128 + i * 32, 32), 32)
+            at = pl.ds(pl.multiple_of(tile * TILE + i * 32, 32), 32)
             moved = MOMENTUM_DECAY * moments[at, :] + factor * grads[at, :]
             new_moments[at, :] = moved
             new_weights[at, :] = (weights[at, :].astype(jnp.float32) - STEP_RATE * moved).astype(
@@ -472,10 +477,11 @@
             )
             return carry
 
-        lax.fori_loop(0, 4, chunk, 0)
-        rows = pl.ds(tile * 128, 128)
-        there = rows if tile < 7 else pl.ds(0, 128)
-        outs = (expert_weight_out, expert_moment_out) if tile < 7 else (value_weight_out, value_moment_out)
+        lax.fori_loop(0, TILE // 32, chunk, 0)
+        rows = pl.ds(tile * TILE, TILE)
+        expert = tile * TILE < 896
+        there = rows if expert else pl.ds(tile * TILE - 896, TILE)
+        outs = (expert_weight_out, expert_moment_out) if expert else (value_weight_out, value_moment_out)
         for src, dst, sem in (
             (new_weights, outs[0], weight_sem),
             (new_moments, outs[1], moment_sem),
@@ -521,7 +527,7 @@
             pltpu.VMEM((128, 1024), bf16),
             pltpu.VMEM((2, 128, 1024), bf16),
             pltpu.VMEM((128, 1024), bf16),
-            pltpu.VMEM((25, 8, 128), jnp.float32),
+            pltpu.VMEM((25, 1, 128), jnp.float32),
             dma((16,)),
             dma((2,)), dma((2,)),
             dma((9,)), dma((9,)),
@@ -566,8 +572,8 @@
         scratch_shapes=[
             pltpu.VMEM((1024, 1024), bf16),
             pltpu.VMEM((1024, 1024), jnp.float32),
-            dma((8,)),
-            dma((8,)),
+            dma((1024 // TILE,)),
+            dma((1024 // TILE,)),
         ],
         compiler_params=pltpu.CompilerParams(vmem_limit_bytes=24 * 1024 * 1024),
         cost_estimate=pl.CostEstimate(flops=6 * 1024 * 1024, bytes_accessed=6_000_000, transcendentals=0),

time: 102 us -> 101 us (level)
  no operation moved by 1% of the time
where the time goes in v6:
time: 101 us
  Pallas kernels  100 us (99%)
    pallas_call x1, Pallas kernels, on_device(): pl.pallas_call(kernel, name='gradients', out_shape=(pltpu.VMEM((1024, 102...  97.2 us
    pallas_call x1, Pallas kernels, on_device(): pl.pallas_call(update_kernel, name='update', out_shape=(jax.ShapeDtypeStr...  3.05 us

profile of v6, /device:TPU:1, one launch (start us, length us, event | category | flops | bytes accessed | tf_op | source)
XLA Modules:
  0.0 100.9 jit_solution(16250588681207672004)
XLA Ops:
  0.6 97.2 %gradients.1 = (f32[1024,1024]{1,0:T(8,128)S(1)}, f32[1024,1024]{1,0:T(8,128)S(1)}, bf16[1024,1024]{1,0:T(8,128)(2,1)S(1)}, f32[8,128]{1,0:T(8,128)S(1)}) custom-call(s32[4]{0:T(128)} %bitcast.27, bf16[4,32]{1,0:T(4,128)(2,1)} %bitcast.26, bf16[384,4096]{1,0:T(8,128)(2,1)} %bitcast.16, bf16[384,1024]{1,0:T(8,128)(2,1)} %bitcast.21, ...), custom_call_target="tpu_custom_call" | custom-call | flops 10737418240 | bytes 10000000 | tf_op jit(solution)/shard_map/gradients/pallas_call | solution.py:504
  97.9 3.1 %update.1 = (bf16[896,1024]{1,0:T(8,128)(2,1)}, f32[896,1024]{1,0:T(8,128)}, bf16[128,1024]{1,0:T(8,128)(2,1)}, f32[128,1024]{1,0:T(8,128)}) custom-call(f32[8,128]{1,0:T(8,128)S(1)} %get-tuple-element.12.factor_ref, f32[1024,1024]{1,0:T(8,128)S(1)} %get-tuple-element.13.grads, f32[1024,1024]{1,0:T(8,128)S(1)} %get-tuple-element.14.moments, ...), custom_call_target="tpu_custom_call" | custom-call | flops 6291456 | bytes 6000000 | tf_op jit(solution)/shard_map/update/pallas_call | solution.py:561

commit v7 on v6

--- a/solution.py
+++ b/solution.py
@@ -273,9 +273,9 @@
 
     def accumulate(weights_of, gathered_of, first=False):
         def tile(n, carry):
-            place = pl.ds(pl.multiple_of(n * 256, 256), 256)
+            place = pl.ds(pl.multiple_of(n * 512, 512), 512)
             lhs = weights_of().reshape(256, 896)
-            rhs = gathered_of(place).reshape(256, 256)
+            rhs = gathered_of(place).reshape(256, 512)
             product = lax.dot_general(
                 lhs, rhs, (((0,), (0,)), ((), ())), preferred_element_type=jnp.float32
             )
@@ -285,7 +285,7 @@
                 grads_out[0:896, place] += product
             return carry
 
-        lax.fori_loop(0, 4, tile, 0)
+        lax.fori_loop(0, 2, tile, 0)
 
     def products(slot, replica, first=False):
         accumulate(

time: 101 us -> 101 us (level)
  no operation moved by 1% of the time
where the time goes in v7:
time: 101 us
  Pallas kernels  100 us (99%)
    pallas_call x1, Pallas kernels, on_device(): pl.pallas_call(kernel, name='gradients', out_shape=(pltpu.VMEM((1024, 102...  97.2 us
    pallas_call x1, Pallas kernels, on_device(): pl.pallas_call(update_kernel, name='update', out_shape=(jax.ShapeDtypeStr...  3.05 us

profile of v7, /device:TPU:1, one launch (start us, length us, event | category | flops | bytes accessed | tf_op | source)
XLA Modules:
  0.0 100.9 jit_solution(17273783584805634298)
XLA Ops:
  0.6 97.2 %gradients.1 = (f32[1024,1024]{1,0:T(8,128)S(1)}, f32[1024,1024]{1,0:T(8,128)S(1)}, bf16[1024,1024]{1,0:T(8,128)(2,1)S(1)}, f32[8,128]{1,0:T(8,128)S(1)}) custom-call(s32[4]{0:T(128)} %bitcast.27, bf16[4,32]{1,0:T(4,128)(2,1)} %bitcast.26, bf16[384,4096]{1,0:T(8,128)(2,1)} %bitcast.16, bf16[384,1024]{1,0:T(8,128)(2,1)} %bitcast.21, ...), custom_call_target="tpu_custom_call" | custom-call | flops 10737418240 | bytes 10000000 | tf_op jit(solution)/shard_map/gradients/pallas_call | solution.py:504
  97.9 3.1 %update.1 = (bf16[896,1024]{1,0:T(8,128)(2,1)}, f32[896,1024]{1,0:T(8,128)}, bf16[128,1024]{1,0:T(8,128)(2,1)}, f32[128,1024]{1,0:T(8,128)}) custom-call(f32[8,128]{1,0:T(8,128)S(1)} %get-tuple-element.12.factor_ref, f32[1024,1024]{1,0:T(8,128)S(1)} %get-tuple-element.13.grads, f32[1024,1024]{1,0:T(8,128)S(1)} %get-tuple-element.14.moments, ...), custom_call_target="tpu_custom_call" | custom-call | flops 6291456 | bytes 6000000 | tf_op jit(solution)/shard_map/update/pallas_call | solution.py:561
